TPU v7x, 128 devices: a whole 4x4x4 slice. The times are simulated.
128 devices in a mesh: gx: 4 (over x), gy: 4 (over z), gz: 8 (over y, core).
Axes of the slice: x: 4, y: 4, z: 4, core: 2. Of those that a mesh axis runs over, the one named last changes fastest.
Arguments:
- a_blocks: float32 [6656, 7, 128, 128], P(('gx', 'gy', 'gz')), as said below
- block_cols: int32 [6656, 7], P(('gx', 'gy', 'gz')), may hold values from 0 to 363, as said below
- agg_ids: int32 [6656], P(('gx', 'gy', 'gz')), may hold values from 0 to 51, as said below
- agg_counts: int32 [128], P(('gx', 'gy', 'gz')), may hold values from 1 to 52, as said below
- p0_blocks: float32 [6656, 6, 128], P(('gx', 'gy', 'gz')), may hold values from -6 to 6
- start_vec: float32 [6656, 128], P(('gx', 'gy', 'gz'))
Outputs:
- p_blocks: float32 [6656, 7, 6, 128], P(('gx', 'gy', 'gz'))
- p_cols: int32 [6656, 7], P(('gx', 'gy', 'gz'))
- power_vec: float32 [6656, 128], P(('gx', 'gy', 'gz'))
Inputs may be any that keep to these rules, and one draw needn't show every extreme that they name: `block_cols`: entry 0 of each block row names the row itself; every neighbour that an entry names exists. `agg_ids`: below the count of the row's own subdomain. `agg_counts`: some subdomain has 52 aggregates. `a_blocks`: block 0 of each block row has a positive diagonal.
All inputs are finite; a program needn't handle non-finite values.
Results may differ from a plain program's by a relative error of at most 0.0003.
Values sent between devices are 32-bit elements; how exact they have to be, the bound alone decides.
A program may use at most 128 MiB of HBM per device.

v0:
```python
import jax
import jax.numpy as jnp
from jax import lax
from jax.sharding import Mesh
from jax.sharding import PartitionSpec as P

ITERS = 8
GZ = ("gz_0", "gz_1")
GX_GY_GZ = ("gx", "gy", "gz_0", "gz_1")


precise_mode = lax.Precision.HIGHEST


def sent_to_all(array, axis):
    copies = jnp.broadcast_to(array, (lax.axis_size(axis), *array.shape))
    return lax.all_to_all(copies, axis, split_axis=0, concat_axis=0, tiled=True)


def joined_by_halves(pieces, combine):
    while len(jax.tree.leaves(pieces)[0]) > 1:
        pieces = jax.vmap(combine)(*(pieces[side::2] for side in (0, 1)))
    return pieces[0]


def prefix(array, axis, combine, identity):
    length, position = (lax.axis_size(axis), lax.axis_index(axis))
    passed = jnp.arange(length) < position

    def kept(part, zero, own):
        part = jnp.where(
            passed.reshape(-1, *(1 for _ in own.shape)), part, jnp.asarray(zero, own.dtype)
        )
        return part

    pieces = sent_to_all(array, axis)
    return joined_by_halves(kept(pieces, identity, array), combine)


def taken_together(array, axis):
    return sent_to_all(array, axis).sum(axis=0)


def extended(array, sides, width):
    edges = {}
    for axis, dim in sides:
        size, length = (lax.axis_size(axis), array.shape[dim])
        up = [(i, (i + 1) % size) for i in range(size - 1)]
        last = lax.slice_in_dim(array, length - width, length, axis=dim)
        leading = lax.slice_in_dim(array, 0, width, axis=dim)
        edges[dim] = (
            lax.ppermute(last, axis, up),
            lax.ppermute(leading, axis, [(b, a) for a, b in up]),
        )
    done = []
    for _, dim in sides:
        low, high = edges[dim]
        around = [(width, width) if d in done else (0, 0) for d in range(array.ndim)]
        array = jnp.concatenate([jnp.pad(low, around), array, jnp.pad(high, around)], axis=dim)
        done.append(dim)
    return array


def by_axis(array, axes):
    for axis in axes:
        array = lax.psum(array, axis)
    return array


def faces_of(wide):
    return jnp.concatenate(
        [
            wide[1, 1, 1],
            wide[0, 1, 1],
            wide[2, 1, 1],
            wide[1, 0, 1],
            wide[1, 2, 1],
            wide[1, 1, 0],
            wide[1, 1, 2],
        ],
        axis=0,
    )


def add_counts(earlier, later):
    return earlier + later


def offset_of(agg_counts):
    empty = jnp.zeros((1,), jnp.int32)
    inner = prefix(agg_counts, GZ, add_counts, empty)
    line_total = taken_together(agg_counts, GZ)
    middle = prefix(line_total, "gy", add_counts, empty)
    plane_total = taken_together(line_total, "gy")
    outer = prefix(plane_total, "gx", add_counts, empty)
    return (inner + middle + outer)[0]


def local(a_blocks, block_cols, agg_ids, agg_counts, p0_blocks, start_vec):
    diag_values = jnp.diagonal(a_blocks[:, 0], axis1=1, axis2=2)
    entry_total = (
        lax.axis_size("gx")
        * lax.axis_size("gy")
        * lax.axis_size(GZ)
        * start_vec.shape[0]
        * start_vec.shape[1]
    )
    root_total = jnp.sqrt(jnp.float32(entry_total))
    previous = start_vec
    current = start_vec
    for turn_index in range(ITERS):
        previous = current
        operate_wide = extended(current[None, None, None], (("gx", 0), ("gy", 1), (GZ, 2)), 1)
        picked = faces_of(operate_wide)[block_cols]
        mixed = jnp.einsum("bkij,bkj->bi", a_blocks, picked, precision=precise_mode)
        current = mixed / diag_values
    totals = (
        by_axis(jnp.sum(previous * previous), GX_GY_GZ),
        by_axis(jnp.sum(current * current), GX_GY_GZ),
    )
    last_norm = jnp.sqrt(totals[1])
    spectral = last_norm / jnp.sqrt(totals[0])
    power_vec = current * (root_total / last_norm)
    damping = 4.0 / (3.0 * spectral)
    wide = extended(p0_blocks[None, None, None], (("gx", 0), ("gy", 1), (GZ, 2)), 1)
    picked_p0 = faces_of(wide)[block_cols]
    product = jnp.einsum("bksj,bkij->bksi", picked_p0, a_blocks, precision=precise_mode)
    smoothed = -(damping / diag_values)[:, None, None, :] * product
    p_blocks = smoothed.at[:, 0].add(p0_blocks)
    offset = offset_of(agg_counts)
    own_columns = (p0_blocks.shape[1] * (offset + agg_ids)).astype(jnp.int32)
    wide_columns = extended(own_columns[None, None, None], (("gx", 0), ("gy", 1), (GZ, 2)), 1)
    p_cols = faces_of(wide_columns)[block_cols]
    return (p_blocks, p_cols, power_vec.astype(jnp.float32))


def solution(mesh):
    split = Mesh(
        mesh.devices.reshape(mesh.shape["gx"], mesh.shape["gy"], 4, 2), ("gx", "gy", "gz_0", "gz_1")
    )
    placed = (
        P(GX_GY_GZ, None, None, None),
        P(GX_GY_GZ, None),
        P(GX_GY_GZ),
        P(GX_GY_GZ),
        P(GX_GY_GZ, None, None),
        P(GX_GY_GZ, None),
    )
    return jax.shard_map(
        local,
        mesh=split,
        in_specs=placed,
        out_specs=(P(GX_GY_GZ, None, None, None), P(GX_GY_GZ, None), P(GX_GY_GZ, None)),
        check_vma=False,
    )
```

profile of v0, /device:TPU:0, one launch (start us, length us, event | category | flops | bytes accessed | tf_op | source)
XLA Modules:
  0.0 518.7 jit_solution(12061031796997480983)
XLA Ops:
  0.6 3.5 collective-permute-start
  4.1 1.3 collective-permute-start.1
  5.4 3.8 collective-permute-start.2
  10.6 1.9 collective-permute-start.4
  13.7 5.5 %all-to-all-start = ((s32[8,1,1]{2,1,0:T(1,128)}), s32[8,1,1]{2,1,0:T(1,128)S(1)}, u32[]{:S(2)}, u32[]{:S(2)}) async-start(s32[8,1,1]{2,1,0:T(1,128)} %broadcast_in_dim.77), calls=%async_computation | async-start | bytes 8192 | tf_op jit(solution)/shard_map/all_to_all | solution.py:17
  20.2 2.0 slice-done
  22.1 4.8 copy.103
  27.0 1.8 gather_fusion.1
  28.9 1.3 collective-permute-start.5
  32.0 1.8 concatenate.36
  35.1 24.7 %fusion.8 = f32[52,1,128,1]{2,1,3,0:T(1,128)S(1)} fusion(f32[52,7,128,1]{2,3,1,0:T(1,128)S(1)} %reshape.251, f32[52,7,128,128]{3,2,1,0:T(8,128)} %param.8), kind=kOutput, calls=%fused_computation.48 | convolution fusion | flops 71565312 | bytes 24068096 | tf_op jit(solution)/shard_map/bkij,bkj->bi/dot_general | solution.py:115
  59.9 4.5 collective-permute-start.6
  66.1 4.6 collective-permute-start.8
  72.0 3.9 collective-permute-start.10
  79.0 6.9 %all-to-all-start.1 = ((s32[4,1,1]{2,1,0:T(1,128)}), s32[4,1,1]{2,1,0:T(1,128)S(1)}, u32[]{:S(2)}, u32[]{:S(2)}) async-start(s32[4,1,1]{2,1,0:T(1,128)} %broadcast_in_dim.79), calls=%async_computation.1 | async-start | bytes 4096 | tf_op jit(solution)/shard_map/all_to_all | solution.py:17
  89.0 24.7 %fusion.9 = f32[52,1,128,1]{2,1,3,0:T(1,128)S(1)} fusion(f32[52,7,128,1]{2,3,1,0:T(1,128)S(1)} %reshape.253, f32[52,7,128,128]{3,2,1,0:T(8,128)} %param.8), kind=kOutput, calls=%fused_computation.49 | convolution fusion | flops 71565312 | bytes 24068096 | tf_op jit(solution)/shard_map/bkij,bkj->bi/dot_general | solution.py:115
  113.8 4.3 collective-permute-start.12
  120.1 3.9 collective-permute-start.14
  125.3 2.5 collective-permute-start.16
  129.8 3.5 collective-permute-done.17
  135.0 24.7 %fusion.10 = f32[52,1,128,1]{2,1,3,0:T(1,128)S(1)} fusion(f32[52,7,128,1]{2,3,1,0:T(1,128)S(1)} %reshape.255, f32[52,7,128,128]{3,2,1,0:T(8,128)} %param.8), kind=kOutput, calls=%fused_computation.50 | convolution fusion | flops 71565312 | bytes 24068096 | tf_op jit(solution)/shard_map/bkij,bkj->bi/dot_general | solution.py:115
  159.8 4.5 collective-permute-start.18
  166.2 4.0 all-to-all-start.2
  171.5 3.9 all-to-all-done.2
  176.8 4.5 collective-permute-start.20
  181.4 1.3 collective-permute-start.21
  182.7 2.5 collective-permute-start.22
  185.2 1.5 collective-permute-start.23
  187.2 2.6 collective-permute-done.23
  191.6 24.7 %fusion.11 = f32[52,1,128,1]{2,1,3,0:T(1,128)S(1)} fusion(f32[52,7,128,1]{2,3,1,0:T(1,128)S(1)} %reshape.257, f32[52,7,128,128]{3,2,1,0:T(8,128)} %param.8), kind=kOutput, calls=%fused_computation.51 | convolution fusion | flops 71565312 | bytes 24068096 | tf_op jit(solution)/shard_map/bkij,bkj->bi/dot_general | solution.py:115
  216.3 4.5 collective-permute-start.24
  224.1 4.5 collective-permute-start.26
  229.9 3.9 collective-permute-start.28
  233.9 1.3 collective-permute-start.29
  235.2 4.3 collective-permute-start.54
  241.3 24.8 %fusion.12 = f32[52,1,128,1]{2,1,3,0:T(1,128)S(1)} fusion(f32[52,7,128,1]{2,3,1,0:T(1,128)S(1)} %reshape.259, f32[52,7,128,128]{3,2,1,0:T(8,128)} %param.8), kind=kOutput, calls=%fused_computation.52 | convolution fusion | flops 71565312 | bytes 24068096 | tf_op jit(solution)/shard_map/bkij,bkj->bi/dot_general | solution.py:115
  266.1 2.5 collective-permute-start.30
  270.0 4.3 collective-permute-start.56
  275.6 3.7 collective-permute-start.58
  279.3 1.3 collective-permute-start.59
  281.9 4.3 collective-permute-start.32
  287.5 4.2 collective-permute-start.34
  291.7 1.5 collective-permute-start.35
  293.3 2.8 gather_fusion.10
  296.9 5.2 collective-permute-start.48
  303.4 4.3 collective-permute-start.50
  307.7 1.3 collective-permute-start.51
  310.8 24.7 %fusion.13 = f32[52,1,128,1]{2,1,3,0:T(1,128)S(1)} fusion(f32[52,7,128,1]{2,3,1,0:T(1,128)S(1)} %reshape.261, f32[52,7,128,128]{3,2,1,0:T(8,128)} %param.8), kind=kOutput, calls=%fused_computation.53 | convolution fusion | flops 71565312 | bytes 24068096 | tf_op jit(solution)/shard_map/bkij,bkj->bi/dot_general | solution.py:115
  335.6 4.5 collective-permute-start.36
  341.5 4.5 collective-permute-start.38
  347.4 3.4 collective-permute-start.40
  352.2 5.7 %collective-permute-start.52 = (f32[1,1,1,52,6,128]{5,4,3,2,1,0:T(8,128)S(1)}, f32[1,1,1,52,6,128]{5,4,3,2,1,0:T(8,128)S(1)}, u32[]{:S(2)}, u32[]{:S(2)}) collective-permute-start(f32[1,1,1,52,6,128]{5,4,3,2,1,0:T(8,128)S(1)} %get-tuple-element.44), channel_id=1, source_target_pairs={{0,1},{1,2},{2,3},{3,4},{4,5},{5,6},{6,7},{8,9},{9,10},{10,11},{11... | collective-permute-start | bytes 479240 | tf_op jit(solution)/shard_map/ppermute | solution.py:52
  361.0 24.7 %fusion.14 = f32[52,1,128,1]{2,1,3,0:T(1,128)S(1)} fusion(f32[52,7,128,1]{2,3,1,0:T(1,128)S(1)} %reshape.263, f32[52,7,128,128]{3,2,1,0:T(8,128)} %param.8), kind=kOutput, calls=%fused_computation.54 | convolution fusion | flops 71565312 | bytes 24068096 | tf_op jit(solution)/shard_map/bkij,bkj->bi/dot_general | solution.py:115
  386.4 4.5 collective-permute-start.42
  392.3 5.0 collective-permute-start.44
  398.5 3.7 collective-permute-start.46
  403.6 2.1 gather_fusion.9
  405.7 1.5 collective-permute-done.47
  408.9 24.7 %fusion.15 = f32[52,1,128,1]{2,1,3,0:T(1,128)S(1)} fusion(f32[52,7,128,1]{2,3,1,0:T(1,128)S(1)} %reshape.265, f32[52,7,128,128]{3,2,1,0:T(8,128)} %param.8), kind=kOutput, calls=%fused_computation.55 | convolution fusion | flops 71565312 | bytes 24068096 | tf_op jit(solution)/shard_map/bkij,bkj->bi/dot_general | solution.py:115
  434.2 12.1 %all-reduce.2 = (f32[]{:T(128)}, f32[]{:T(128)}) all-reduce(f32[]{:T(128)} %multiply_reduce_fusion.1, f32[]{:T(128)} %get-tuple-element.42), channel_id=1, replica_groups=mesh['gx'=4,'gy'=4,'gz_0'=4,'gz_1'=2] {'gx'}, use_global_device_ids=true, to_apply=%region_1.2 | all-reduce | flops 2 | bytes 16 | tf_op jit(solution)/shard_map/psum | solution.py:66
  446.4 12.2 %all-reduce.1 = (f32[]{:T(128)}, f32[]{:T(128)}) all-reduce(f32[]{:T(128)} %get-tuple-element.38, f32[]{:T(128)} %get-tuple-element.39), channel_id=1, replica_groups=mesh['gx'=4,'gy'=4,'gz_0'=4,'gz_1'=2] {'gy'}, use_global_device_ids=true, to_apply=%region_2.3 | all-reduce | flops 2 | bytes 16 | tf_op jit(solution)/shard_map/psum | solution.py:66
  458.6 13.2 %all-reduce = (f32[]{:T(128)}, f32[]{:T(128)}) all-reduce(f32[]{:T(128)} %get-tuple-element.36, f32[]{:T(128)} %get-tuple-element.37), channel_id=1, replica_groups=mesh['gx'=4,'gy'=4,'gz_0'=4,'gz_1'=2] {'gz_0'}, use_global_device_ids=true, to_apply=%region_3.4 | all-reduce | flops 2 | bytes 16 | tf_op jit(solution)/shard_map/psum | solution.py:66
  471.7 3.3 all-reduce.3
  477.1 40.1 %convolution_multiply_fusion = f32[52,7,6,128]{3,2,1,0:T(8,128)S(1)} fusion(f32[52,7,6,128]{3,2,1,0:T(8,128)S(1)} %bitcast.153, f32[52,7,128,128]{3,2,1,0:T(8,128)} %param.8, f32[52,128]{1,0:T(8,128)S(1)} %get-tuple-element.47), kind=kOutput, calls=%fused_computation.11 | convolution fusion | flops 429671424 | bytes 26118144 | tf_op jit(solution)/shard_map/bksj,bkij->bksi/dot_general | solution.py:127
  (166 shorter events, 56.3 us)
Async XLA Ops:
  0.6 28.2 %collective-permute-start = (f32[1,1,1,52,128]{4,3,2,1,0:T(8,128)}, f32[1,1,1,52,128]{4,3,2,1,0:T(8,128)S(1)}, u32[]{:S(2)}, u32[]{:S(2)}) collective-permute-start(f32[1,1,1,52,128]{4,3,2,1,0:T(8,128)} %bitcast.197), channel_id=1, source_target_pairs={{0,32},{32,64},{64,96},{1,33},{33,65},{65,97},{2,34},{34,66},{66,9... | collective-permute-start | bytes 79880 | tf_op jit(solution)/shard_map/ppermute | solution.py:52
  4.1 26.8 %collective-permute-start.1 = (f32[1,1,1,52,128]{4,3,2,1,0:T(8,128)}, f32[1,1,1,52,128]{4,3,2,1,0:T(8,128)S(1)}, u32[]{:S(2)}, u32[]{:S(2)}) collective-permute-start(f32[1,1,1,52,128]{4,3,2,1,0:T(8,128)} %bitcast.198), channel_id=1, source_target_pairs={{32,0},{64,32},{96,64},{33,1},{65,33},{97,65},{34,2},{66,34},{98,6... | collective-permute-start | bytes 79880 | tf_op jit(solution)/shard_map/ppermute | solution.py:53
  5.4 25.5 %collective-permute-start.2 = (f32[1,1,1,52,128]{4,3,2,1,0:T(8,128)}, f32[1,1,1,52,128]{4,3,2,1,0:T(8,128)S(1)}, u32[]{:S(2)}, u32[]{:S(2)}) collective-permute-start(f32[1,1,1,52,128]{4,3,2,1,0:T(8,128)} %bitcast.199), channel_id=1, source_target_pairs={{0,8},{8,16},{16,24},{1,9},{9,17},{17,25},{2,10},{10,18},{18,26},{... | collective-permute-start | bytes 79880 | tf_op jit(solution)/shard_map/ppermute | solution.py:52
  9.3 21.7 %collective-permute-start.3 = (f32[1,1,1,52,128]{4,3,2,1,0:T(8,128)}, f32[1,1,1,52,128]{4,3,2,1,0:T(8,128)}, u32[]{:S(2)}, u32[]{:S(2)}) collective-permute-start(f32[1,1,1,52,128]{4,3,2,1,0:T(8,128)} %bitcast.200), channel_id=1, source_target_pairs={{8,0},{16,8},{24,16},{9,1},{17,9},{25,17},{10,2},{18,10},{26,18},{... | collective-permute-start | bytes 79880 | tf_op jit(solution)/shard_map/ppermute | solution.py:53
  10.6 20.4 %collective-permute-start.4 = (f32[1,1,1,52,128]{4,3,2,1,0:T(8,128)}, f32[1,1,1,52,128]{4,3,2,1,0:T(8,128)}, u32[]{:S(2)}, u32[]{:S(2)}) collective-permute-start(f32[1,1,1,52,128]{4,3,2,1,0:T(8,128)} %bitcast.201), channel_id=1, source_target_pairs={{0,1},{1,2},{2,3},{3,4},{4,5},{5,6},{6,7},{8,9},{9,10},{10,11},{11... | collective-permute-start | bytes 79880 | tf_op jit(solution)/shard_map/ppermute | solution.py:52
  13.7 16.4 %all-to-all-start = ((s32[8,1,1]{2,1,0:T(1,128)}), s32[8,1,1]{2,1,0:T(1,128)S(1)}, u32[]{:S(2)}, u32[]{:S(2)}) async-start(s32[8,1,1]{2,1,0:T(1,128)} %broadcast_in_dim.77), calls=%async_computation | async-start | bytes 8192 | tf_op jit(solution)/shard_map/all_to_all | solution.py:17
  28.9 3.1 collective-permute-start.5
  59.9 16.1 %collective-permute-start.6 = (f32[1,1,1,52,128]{4,3,2,1,0:T(8,128)S(1)}, f32[1,1,1,52,128]{4,3,2,1,0:T(8,128)S(1)}, u32[]{:S(2)}, u32[]{:S(2)}) collective-permute-start(f32[1,1,1,52,128]{4,3,2,1,0:T(8,128)S(1)} %bitcast.173), channel_id=1, source_target_pairs={{0,32},{32,64},{64,96},{1,33},{33,65},{65,97},{2,34},{34,66},{66,9... | collective-permute-start | bytes 79880 | tf_op jit(solution)/shard_map/ppermute | solution.py:52
  64.8 22.4 %collective-permute-start.7 = (f32[1,1,1,52,128]{4,3,2,1,0:T(8,128)S(1)}, f32[1,1,1,52,128]{4,3,2,1,0:T(8,128)S(1)}, u32[]{:S(2)}, u32[]{:S(2)}) collective-permute-start(f32[1,1,1,52,128]{4,3,2,1,0:T(8,128)S(1)} %bitcast.174), channel_id=1, source_target_pairs={{32,0},{64,32},{96,64},{33,1},{65,33},{97,65},{34,2},{66,34},{98,6... | collective-permute-start | bytes 79880 | tf_op jit(solution)/shard_map/ppermute | solution.py:53
  66.1 21.1 %collective-permute-start.8 = (f32[1,1,1,52,128]{4,3,2,1,0:T(8,128)S(1)}, f32[1,1,1,52,128]{4,3,2,1,0:T(8,128)S(1)}, u32[]{:S(2)}, u32[]{:S(2)}) collective-permute-start(f32[1,1,1,52,128]{4,3,2,1,0:T(8,128)S(1)} %bitcast.175), channel_id=1, source_target_pairs={{0,8},{8,16},{16,24},{1,9},{9,17},{17,25},{2,10},{10,18},{18,26},{... | collective-permute-start | bytes 79880 | tf_op jit(solution)/shard_map/ppermute | solution.py:52
  70.7 16.5 %collective-permute-start.9 = (f32[1,1,1,52,128]{4,3,2,1,0:T(8,128)S(1)}, f32[1,1,1,52,128]{4,3,2,1,0:T(8,128)S(1)}, u32[]{:S(2)}, u32[]{:S(2)}) collective-permute-start(f32[1,1,1,52,128]{4,3,2,1,0:T(8,128)S(1)} %bitcast.176), channel_id=1, source_target_pairs={{8,0},{16,8},{24,16},{9,1},{17,9},{25,17},{10,2},{18,10},{26,18},{... | collective-permute-start | bytes 79880 | tf_op jit(solution)/shard_map/ppermute | solution.py:53
  72.0 15.2 %collective-permute-start.10 = (f32[1,1,1,52,128]{4,3,2,1,0:T(8,128)S(1)}, f32[1,1,1,52,128]{4,3,2,1,0:T(8,128)S(1)}, u32[]{:S(2)}, u32[]{:S(2)}) collective-permute-start(f32[1,1,1,52,128]{4,3,2,1,0:T(8,128)S(1)} %bitcast.177), channel_id=1, source_target_pairs={{0,1},{1,2},{2,3},{3,4},{4,5},{5,6},{6,7},{8,9},{9,10},{10,11},{11... | collective-permute-start | bytes 79880 | tf_op jit(solution)/shard_map/ppermute | solution.py:52
  75.9 11.3 %collective-permute-start.11 = (f32[1,1,1,52,128]{4,3,2,1,0:T(8,128)S(1)}, f32[1,1,1,52,128]{4,3,2,1,0:T(8,128)S(1)}, u32[]{:S(2)}, u32[]{:S(2)}) collective-permute-start(f32[1,1,1,52,128]{4,3,2,1,0:T(8,128)S(1)} %bitcast.178), channel_id=1, source_target_pairs={{1,0},{2,1},{3,2},{4,3},{5,4},{6,5},{7,6},{9,8},{10,9},{11,10},{12... | collective-permute-start | bytes 79880 | tf_op jit(solution)/shard_map/ppermute | solution.py:53
  79.0 39.0 %all-to-all-start.1 = ((s32[4,1,1]{2,1,0:T(1,128)}), s32[4,1,1]{2,1,0:T(1,128)S(1)}, u32[]{:S(2)}, u32[]{:S(2)}) async-start(s32[4,1,1]{2,1,0:T(1,128)} %broadcast_in_dim.79), calls=%async_computation.1 | async-start | bytes 4096 | tf_op jit(solution)/shard_map/all_to_all | solution.py:17
  113.8 14.1 %collective-permute-start.12 = (f32[1,1,1,52,128]{4,3,2,1,0:T(8,128)S(1)}, f32[1,1,1,52,128]{4,3,2,1,0:T(8,128)S(1)}, u32[]{:S(2)}, u32[]{:S(2)}) collective-permute-start(f32[1,1,1,52,128]{4,3,2,1,0:T(8,128)S(1)} %bitcast.179), channel_id=1, source_target_pairs={{0,32},{32,64},{64,96},{1,33},{33,65},{65,97},{2,34},{34,66},{66,9... | collective-permute-start | bytes 79880 | tf_op jit(solution)/shard_map/ppermute | solution.py:52
  118.8 10.6 %collective-permute-start.13 = (f32[1,1,1,52,128]{4,3,2,1,0:T(8,128)S(1)}, f32[1,1,1,52,128]{4,3,2,1,0:T(8,128)S(1)}, u32[]{:S(2)}, u32[]{:S(2)}) collective-permute-start(f32[1,1,1,52,128]{4,3,2,1,0:T(8,128)S(1)} %bitcast.180), channel_id=1, source_target_pairs={{32,0},{64,32},{96,64},{33,1},{65,33},{97,65},{34,2},{66,34},{98,6... | collective-permute-start | bytes 79880 | tf_op jit(solution)/shard_map/ppermute | solution.py:53
  120.1 9.3 %collective-permute-start.14 = (f32[1,1,1,52,128]{4,3,2,1,0:T(8,128)S(1)}, f32[1,1,1,52,128]{4,3,2,1,0:T(8,128)S(1)}, u32[]{:S(2)}, u32[]{:S(2)}) collective-permute-start(f32[1,1,1,52,128]{4,3,2,1,0:T(8,128)S(1)} %bitcast.181), channel_id=1, source_target_pairs={{0,8},{8,16},{16,24},{1,9},{9,17},{17,25},{2,10},{10,18},{18,26},{... | collective-permute-start | bytes 79880 | tf_op jit(solution)/shard_map/ppermute | solution.py:52
  124.0 5.8 %collective-permute-start.15 = (f32[1,1,1,52,128]{4,3,2,1,0:T(8,128)S(1)}, f32[1,1,1,52,128]{4,3,2,1,0:T(8,128)S(1)}, u32[]{:S(2)}, u32[]{:S(2)}) collective-permute-start(f32[1,1,1,52,128]{4,3,2,1,0:T(8,128)S(1)} %bitcast.182), channel_id=1, source_target_pairs={{8,0},{16,8},{24,16},{9,1},{17,9},{25,17},{10,2},{18,10},{26,18},{... | collective-permute-start | bytes 79880 | tf_op jit(solution)/shard_map/ppermute | solution.py:53
  125.3 4.5 collective-permute-start.16
  127.8 5.5 %collective-permute-start.17 = (f32[1,1,1,52,128]{4,3,2,1,0:T(8,128)S(1)}, f32[1,1,1,52,128]{4,3,2,1,0:T(8,128)S(1)}, u32[]{:S(2)}, u32[]{:S(2)}) collective-permute-start(f32[1,1,1,52,128]{4,3,2,1,0:T(8,128)S(1)} %bitcast.184), channel_id=1, source_target_pairs={{1,0},{2,1},{3,2},{4,3},{5,4},{6,5},{7,6},{9,8},{10,9},{11,10},{12... | collective-permute-start | bytes 79880 | tf_op jit(solution)/shard_map/ppermute | solution.py:53
  159.8 25.4 %collective-permute-start.18 = (f32[1,1,1,52,128]{4,3,2,1,0:T(8,128)S(1)}, f32[1,1,1,52,128]{4,3,2,1,0:T(8,128)S(1)}, u32[]{:S(2)}, u32[]{:S(2)}) collective-permute-start(f32[1,1,1,52,128]{4,3,2,1,0:T(8,128)S(1)} %bitcast.161), channel_id=1, source_target_pairs={{0,32},{32,64},{64,96},{1,33},{33,65},{65,97},{2,34},{34,66},{66,9... | collective-permute-start | bytes 79880 | tf_op jit(solution)/shard_map/ppermute | solution.py:52
  166.2 9.2 %all-to-all-start.2 = ((s32[4,1,1]{2,1,0:T(1,128)}), s32[4,1,1]{2,1,0:T(1,128)S(1)}, u32[]{:S(2)}, u32[]{:S(2)}) async-start(s32[4,1,1]{2,1,0:T(1,128)} %broadcast_in_dim.81), calls=%async_computation.2 | async-start | bytes 4096 | tf_op jit(solution)/shard_map/all_to_all | solution.py:17
  175.5 11.4 %collective-permute-start.19 = (f32[1,1,1,52,128]{4,3,2,1,0:T(8,128)S(1)}, f32[1,1,1,52,128]{4,3,2,1,0:T(8,128)S(1)}, u32[]{:S(2)}, u32[]{:S(2)}) collective-permute-start(f32[1,1,1,52,128]{4,3,2,1,0:T(8,128)S(1)} %bitcast.162), channel_id=1, source_target_pairs={{32,0},{64,32},{96,64},{33,1},{65,33},{97,65},{34,2},{66,34},{98,6... | collective-permute-start | bytes 79880 | tf_op jit(solution)/shard_map/ppermute | solution.py:53
  176.8 10.1 %collective-permute-start.20 = (f32[1,1,1,52,128]{4,3,2,1,0:T(8,128)S(1)}, f32[1,1,1,52,128]{4,3,2,1,0:T(8,128)S(1)}, u32[]{:S(2)}, u32[]{:S(2)}) collective-permute-start(f32[1,1,1,52,128]{4,3,2,1,0:T(8,128)S(1)} %bitcast.163), channel_id=1, source_target_pairs={{0,8},{8,16},{16,24},{1,9},{9,17},{17,25},{2,10},{10,18},{18,26},{... | collective-permute-start | bytes 79880 | tf_op jit(solution)/shard_map/ppermute | solution.py:52
  181.4 5.8 %collective-permute-start.21 = (f32[1,1,1,52,128]{4,3,2,1,0:T(8,128)S(1)}, f32[1,1,1,52,128]{4,3,2,1,0:T(8,128)S(1)}, u32[]{:S(2)}, u32[]{:S(2)}) collective-permute-start(f32[1,1,1,52,128]{4,3,2,1,0:T(8,128)S(1)} %bitcast.164), channel_id=1, source_target_pairs={{8,0},{16,8},{24,16},{9,1},{17,9},{25,17},{10,2},{18,10},{26,18},{... | collective-permute-start | bytes 79880 | tf_op jit(solution)/shard_map/ppermute | solution.py:53
  182.7 4.5 collective-permute-start.22
  185.2 4.6 collective-permute-start.23
  191.6 43.6 %copy-start.3 = (s32[52]{0:T(128)S(1)}, s32[52]{0:T(128)}, u32[]{:S(2)}) copy-start(s32[52]{0:T(128)} %param.10) | copy-start | bytes 628
  216.3 17.5 %collective-permute-start.24 = (f32[1,1,1,52,128]{4,3,2,1,0:T(8,128)S(1)}, f32[1,1,1,52,128]{4,3,2,1,0:T(8,128)S(1)}, u32[]{:S(2)}, u32[]{:S(2)}) collective-permute-start(f32[1,1,1,52,128]{4,3,2,1,0:T(8,128)S(1)} %bitcast.191), channel_id=1, source_target_pairs={{0,32},{32,64},{64,96},{1,33},{33,65},{65,97},{2,34},{34,66},{66,9... | collective-permute-start | bytes 79880 | tf_op jit(solution)/shard_map/ppermute | solution.py:52
  222.8 12.4 %collective-permute-start.25 = (f32[1,1,1,52,128]{4,3,2,1,0:T(8,128)S(1)}, f32[1,1,1,52,128]{4,3,2,1,0:T(8,128)S(1)}, u32[]{:S(2)}, u32[]{:S(2)}) collective-permute-start(f32[1,1,1,52,128]{4,3,2,1,0:T(8,128)S(1)} %bitcast.192), channel_id=1, source_target_pairs={{32,0},{64,32},{96,64},{33,1},{65,33},{97,65},{34,2},{66,34},{98,6... | collective-permute-start | bytes 79880 | tf_op jit(solution)/shard_map/ppermute | solution.py:53
  224.1 15.4 %collective-permute-start.26 = (f32[1,1,1,52,128]{4,3,2,1,0:T(8,128)S(1)}, f32[1,1,1,52,128]{4,3,2,1,0:T(8,128)S(1)}, u32[]{:S(2)}, u32[]{:S(2)}) collective-permute-start(f32[1,1,1,52,128]{4,3,2,1,0:T(8,128)S(1)} %bitcast.193), channel_id=1, source_target_pairs={{0,8},{8,16},{16,24},{1,9},{9,17},{17,25},{2,10},{10,18},{18,26},{... | collective-permute-start | bytes 79880 | tf_op jit(solution)/shard_map/ppermute | solution.py:52
  228.6 10.9 %collective-permute-start.27 = (f32[1,1,1,52,128]{4,3,2,1,0:T(8,128)S(1)}, f32[1,1,1,52,128]{4,3,2,1,0:T(8,128)S(1)}, u32[]{:S(2)}, u32[]{:S(2)}) collective-permute-start(f32[1,1,1,52,128]{4,3,2,1,0:T(8,128)S(1)} %bitcast.194), channel_id=1, source_target_pairs={{8,0},{16,8},{24,16},{9,1},{17,9},{25,17},{10,2},{18,10},{26,18},{... | collective-permute-start | bytes 79880 | tf_op jit(solution)/shard_map/ppermute | solution.py:53
  229.9 9.6 %collective-permute-start.28 = (f32[1,1,1,52,128]{4,3,2,1,0:T(8,128)S(1)}, f32[1,1,1,52,128]{4,3,2,1,0:T(8,128)S(1)}, u32[]{:S(2)}, u32[]{:S(2)}) collective-permute-start(f32[1,1,1,52,128]{4,3,2,1,0:T(8,128)S(1)} %bitcast.195), channel_id=1, source_target_pairs={{0,1},{1,2},{2,3},{3,4},{4,5},{5,6},{6,7},{8,9},{9,10},{10,11},{11... | collective-permute-start | bytes 79880 | tf_op jit(solution)/shard_map/ppermute | solution.py:52
  233.9 5.6 %collective-permute-start.29 = (f32[1,1,1,52,128]{4,3,2,1,0:T(8,128)S(1)}, f32[1,1,1,52,128]{4,3,2,1,0:T(8,128)S(1)}, u32[]{:S(2)}, u32[]{:S(2)}) collective-permute-start(f32[1,1,1,52,128]{4,3,2,1,0:T(8,128)S(1)} %bitcast.196), channel_id=1, source_target_pairs={{1,0},{2,1},{3,2},{4,3},{5,4},{6,5},{7,6},{9,8},{10,9},{11,10},{12... | collective-permute-start | bytes 79880 | tf_op jit(solution)/shard_map/ppermute | solution.py:53
  235.2 40.3 %collective-permute-start.54 = (s32[1,1,1,52]{3,2,1,0:T(1,128)S(1)}, s32[1,1,1,52]{3,2,1,0:T(1,128)S(1)}, u32[]{:S(2)}, u32[]{:S(2)}) collective-permute-start(s32[1,1,1,52]{3,2,1,0:T(1,128)S(1)} %fusion.34), channel_id=1, source_target_pairs={{0,32},{32,64},{64,96},{1,33},{33,65},{65,97},{2,34},{34,66},{66,9... | collective-permute-start | bytes 632 | tf_op jit(solution)/shard_map/ppermute | solution.py:52
  266.1 25.6 %collective-permute-start.30 = (f32[1,1,1,52,128]{4,3,2,1,0:T(8,128)S(1)}, f32[1,1,1,52,128]{4,3,2,1,0:T(8,128)S(1)}, u32[]{:S(2)}, u32[]{:S(2)}) collective-permute-start(f32[1,1,1,52,128]{4,3,2,1,0:T(8,128)S(1)} %bitcast.155), channel_id=1, source_target_pairs={{0,32},{32,64},{64,96},{1,33},{33,65},{65,97},{2,34},{34,66},{66,9... | collective-permute-start | bytes 79880 | tf_op jit(solution)/shard_map/ppermute | solution.py:52
  268.7 10.6 %collective-permute-start.55 = (s32[1,1,1,52]{3,2,1,0:T(1,128)S(1)}, s32[1,1,1,52]{3,2,1,0:T(1,128)S(1)}, u32[]{:S(2)}, u32[]{:S(2)}) collective-permute-start(s32[1,1,1,52]{3,2,1,0:T(1,128)S(1)} %fusion.34), channel_id=1, source_target_pairs={{32,0},{64,32},{96,64},{33,1},{65,33},{97,65},{34,2},{66,34},{98,6... | collective-permute-start | bytes 632 | tf_op jit(solution)/shard_map/ppermute | solution.py:53
  270.0 10.7 %collective-permute-start.56 = (s32[1,1,1,52]{3,2,1,0:T(1,128)S(1)}, s32[1,1,1,52]{3,2,1,0:T(1,128)S(1)}, u32[]{:S(2)}, u32[]{:S(2)}) collective-permute-start(s32[1,1,1,52]{3,2,1,0:T(1,128)S(1)} %fusion.34), channel_id=1, source_target_pairs={{0,8},{8,16},{16,24},{1,9},{9,17},{17,25},{2,10},{10,18},{18,26},{... | collective-permute-start | bytes 632 | tf_op jit(solution)/shard_map/ppermute | solution.py:52
  274.2 7.7 %collective-permute-start.57 = (s32[1,1,1,52]{3,2,1,0:T(1,128)S(1)}, s32[1,1,1,52]{3,2,1,0:T(1,128)S(1)}, u32[]{:S(2)}, u32[]{:S(2)}) collective-permute-start(s32[1,1,1,52]{3,2,1,0:T(1,128)S(1)} %fusion.34), channel_id=1, source_target_pairs={{8,0},{16,8},{24,16},{9,1},{17,9},{25,17},{10,2},{18,10},{26,18},{... | collective-permute-start | bytes 632 | tf_op jit(solution)/shard_map/ppermute | solution.py:53
  275.6 10.7 %collective-permute-start.58 = (s32[1,1,1,52]{3,2,1,0:T(1,128)S(1)}, s32[1,1,1,52]{3,2,1,0:T(1,128)S(1)}, u32[]{:S(2)}, u32[]{:S(2)}) collective-permute-start(s32[1,1,1,52]{3,2,1,0:T(1,128)S(1)} %fusion.34), channel_id=1, source_target_pairs={{0,1},{1,2},{2,3},{3,4},{4,5},{5,6},{6,7},{8,9},{9,10},{10,11},{11... | collective-permute-start | bytes 632 | tf_op jit(solution)/shard_map/ppermute | solution.py:52
  279.3 8.2 %collective-permute-start.59 = (s32[1,1,1,52]{3,2,1,0:T(1,128)S(1)}, s32[1,1,1,52]{3,2,1,0:T(1,128)S(1)}, u32[]{:S(2)}, u32[]{:S(2)}) collective-permute-start(s32[1,1,1,52]{3,2,1,0:T(1,128)S(1)} %fusion.34), channel_id=1, source_target_pairs={{1,0},{2,1},{3,2},{4,3},{5,4},{6,5},{7,6},{9,8},{10,9},{11,10},{12... | collective-permute-start | bytes 632 | tf_op jit(solution)/shard_map/ppermute | solution.py:53
  280.6 16.3 %collective-permute-start.31 = (f32[1,1,1,52,128]{4,3,2,1,0:T(8,128)S(1)}, f32[1,1,1,52,128]{4,3,2,1,0:T(8,128)S(1)}, u32[]{:S(2)}, u32[]{:S(2)}) collective-permute-start(f32[1,1,1,52,128]{4,3,2,1,0:T(8,128)S(1)} %bitcast.156), channel_id=1, source_target_pairs={{32,0},{64,32},{96,64},{33,1},{65,33},{97,65},{34,2},{66,34},{98,6... | collective-permute-start | bytes 79880 | tf_op jit(solution)/shard_map/ppermute | solution.py:53
  281.9 20.2 %collective-permute-start.32 = (f32[1,1,1,52,128]{4,3,2,1,0:T(8,128)S(1)}, f32[1,1,1,52,128]{4,3,2,1,0:T(8,128)S(1)}, u32[]{:S(2)}, u32[]{:S(2)}) collective-permute-start(f32[1,1,1,52,128]{4,3,2,1,0:T(8,128)S(1)} %bitcast.157), channel_id=1, source_target_pairs={{0,8},{8,16},{16,24},{1,9},{9,17},{17,25},{2,10},{10,18},{18,26},{... | collective-permute-start | bytes 79880 | tf_op jit(solution)/shard_map/ppermute | solution.py:52
  286.2 17.2 %collective-permute-start.33 = (f32[1,1,1,52,128]{4,3,2,1,0:T(8,128)S(1)}, f32[1,1,1,52,128]{4,3,2,1,0:T(8,128)S(1)}, u32[]{:S(2)}, u32[]{:S(2)}) collective-permute-start(f32[1,1,1,52,128]{4,3,2,1,0:T(8,128)S(1)} %bitcast.158), channel_id=1, source_target_pairs={{8,0},{16,8},{24,16},{9,1},{17,9},{25,17},{10,2},{18,10},{26,18},{... | collective-permute-start | bytes 79880 | tf_op jit(solution)/shard_map/ppermute | solution.py:53
  287.5 20.2 %collective-permute-start.34 = (f32[1,1,1,52,128]{4,3,2,1,0:T(8,128)S(1)}, f32[1,1,1,52,128]{4,3,2,1,0:T(8,128)S(1)}, u32[]{:S(2)}, u32[]{:S(2)}) collective-permute-start(f32[1,1,1,52,128]{4,3,2,1,0:T(8,128)S(1)} %bitcast.159), channel_id=1, source_target_pairs={{0,1},{1,2},{2,3},{3,4},{4,5},{5,6},{6,7},{8,9},{9,10},{10,11},{11... | collective-permute-start | bytes 79880 | tf_op jit(solution)/shard_map/ppermute | solution.py:52
  291.7 17.3 %collective-permute-start.35 = (f32[1,1,1,52,128]{4,3,2,1,0:T(8,128)S(1)}, f32[1,1,1,52,128]{4,3,2,1,0:T(8,128)S(1)}, u32[]{:S(2)}, u32[]{:S(2)}) collective-permute-start(f32[1,1,1,52,128]{4,3,2,1,0:T(8,128)S(1)} %bitcast.160), channel_id=1, source_target_pairs={{1,0},{2,1},{3,2},{4,3},{5,4},{6,5},{7,6},{9,8},{10,9},{11,10},{12... | collective-permute-start | bytes 79880 | tf_op jit(solution)/shard_map/ppermute | solution.py:53
  296.9 43.2 %collective-permute-start.48 = (f32[1,1,1,52,6,128]{5,4,3,2,1,0:T(8,128)S(1)}, f32[1,1,1,52,6,128]{5,4,3,2,1,0:T(8,128)S(1)}, u32[]{:S(2)}, u32[]{:S(2)}) collective-permute-start(f32[1,1,1,52,6,128]{5,4,3,2,1,0:T(8,128)S(1)} %get-tuple-element.44), channel_id=1, source_target_pairs={{0,32},{32,64},{64,96},{1,33},{33,65},{65,97},{2,34},{34,66},{66,9... | collective-permute-start | bytes 479240 | tf_op jit(solution)/shard_map/ppermute | solution.py:52
  302.1 39.4 %collective-permute-start.49 = (f32[1,1,1,52,6,128]{5,4,3,2,1,0:T(8,128)S(1)}, f32[1,1,1,52,6,128]{5,4,3,2,1,0:T(8,128)S(1)}, u32[]{:S(2)}, u32[]{:S(2)}) collective-permute-start(f32[1,1,1,52,6,128]{5,4,3,2,1,0:T(8,128)S(1)} %get-tuple-element.44), channel_id=1, source_target_pairs={{32,0},{64,32},{96,64},{33,1},{65,33},{97,65},{34,2},{66,34},{98,6... | collective-permute-start | bytes 479240 | tf_op jit(solution)/shard_map/ppermute | solution.py:53
  303.4 42.6 %collective-permute-start.50 = (f32[1,1,1,52,6,128]{5,4,3,2,1,0:T(8,128)S(1)}, f32[1,1,1,52,6,128]{5,4,3,2,1,0:T(8,128)S(1)}, u32[]{:S(2)}, u32[]{:S(2)}) collective-permute-start(f32[1,1,1,52,6,128]{5,4,3,2,1,0:T(8,128)S(1)} %get-tuple-element.44), channel_id=1, source_target_pairs={{0,8},{8,16},{16,24},{1,9},{9,17},{17,25},{2,10},{10,18},{18,26},{... | collective-permute-start | bytes 479240 | tf_op jit(solution)/shard_map/ppermute | solution.py:52
  307.7 39.7 %collective-permute-start.51 = (f32[1,1,1,52,6,128]{5,4,3,2,1,0:T(8,128)S(1)}, f32[1,1,1,52,6,128]{5,4,3,2,1,0:T(8,128)S(1)}, u32[]{:S(2)}, u32[]{:S(2)}) collective-permute-start(f32[1,1,1,52,6,128]{5,4,3,2,1,0:T(8,128)S(1)} %get-tuple-element.44), channel_id=1, source_target_pairs={{8,0},{16,8},{24,16},{9,1},{17,9},{25,17},{10,2},{18,10},{26,18},{... | collective-permute-start | bytes 479240 | tf_op jit(solution)/shard_map/ppermute | solution.py:53
  335.6 15.3 %collective-permute-start.36 = (f32[1,1,1,52,128]{4,3,2,1,0:T(8,128)S(1)}, f32[1,1,1,52,128]{4,3,2,1,0:T(8,128)S(1)}, u32[]{:S(2)}, u32[]{:S(2)}) collective-permute-start(f32[1,1,1,52,128]{4,3,2,1,0:T(8,128)S(1)} %bitcast.167), channel_id=1, source_target_pairs={{0,32},{32,64},{64,96},{1,33},{33,65},{65,97},{2,34},{34,66},{66,9... | collective-permute-start | bytes 79880 | tf_op jit(solution)/shard_map/ppermute | solution.py:52
  340.2 12.0 %collective-permute-start.37 = (f32[1,1,1,52,128]{4,3,2,1,0:T(8,128)S(1)}, f32[1,1,1,52,128]{4,3,2,1,0:T(8,128)S(1)}, u32[]{:S(2)}, u32[]{:S(2)}) collective-permute-start(f32[1,1,1,52,128]{4,3,2,1,0:T(8,128)S(1)} %bitcast.168), channel_id=1, source_target_pairs={{32,0},{64,32},{96,64},{33,1},{65,33},{97,65},{34,2},{66,34},{98,6... | collective-permute-start | bytes 79880 | tf_op jit(solution)/shard_map/ppermute | solution.py:53
  341.5 16.4 %collective-permute-start.38 = (f32[1,1,1,52,128]{4,3,2,1,0:T(8,128)S(1)}, f32[1,1,1,52,128]{4,3,2,1,0:T(8,128)S(1)}, u32[]{:S(2)}, u32[]{:S(2)}) collective-permute-start(f32[1,1,1,52,128]{4,3,2,1,0:T(8,128)S(1)} %bitcast.169), channel_id=1, source_target_pairs={{0,8},{8,16},{16,24},{1,9},{9,17},{17,25},{2,10},{10,18},{18,26},{... | collective-permute-start | bytes 79880 | tf_op jit(solution)/shard_map/ppermute | solution.py:52
  346.1 13.1 %collective-permute-start.39 = (f32[1,1,1,52,128]{4,3,2,1,0:T(8,128)S(1)}, f32[1,1,1,52,128]{4,3,2,1,0:T(8,128)S(1)}, u32[]{:S(2)}, u32[]{:S(2)}) collective-permute-start(f32[1,1,1,52,128]{4,3,2,1,0:T(8,128)S(1)} %bitcast.170), channel_id=1, source_target_pairs={{8,0},{16,8},{24,16},{9,1},{17,9},{25,17},{10,2},{18,10},{26,18},{... | collective-permute-start | bytes 79880 | tf_op jit(solution)/shard_map/ppermute | solution.py:53
  347.4 11.8 %collective-permute-start.40 = (f32[1,1,1,52,128]{4,3,2,1,0:T(8,128)S(1)}, f32[1,1,1,52,128]{4,3,2,1,0:T(8,128)S(1)}, u32[]{:S(2)}, u32[]{:S(2)}) collective-permute-start(f32[1,1,1,52,128]{4,3,2,1,0:T(8,128)S(1)} %bitcast.171), channel_id=1, source_target_pairs={{0,1},{1,2},{2,3},{3,4},{4,5},{5,6},{6,7},{8,9},{9,10},{10,11},{11... | collective-permute-start | bytes 79880 | tf_op jit(solution)/shard_map/ppermute | solution.py:52
  350.9 8.4 %collective-permute-start.41 = (f32[1,1,1,52,128]{4,3,2,1,0:T(8,128)S(1)}, f32[1,1,1,52,128]{4,3,2,1,0:T(8,128)S(1)}, u32[]{:S(2)}, u32[]{:S(2)}) collective-permute-start(f32[1,1,1,52,128]{4,3,2,1,0:T(8,128)S(1)} %bitcast.172), channel_id=1, source_target_pairs={{1,0},{2,1},{3,2},{4,3},{5,4},{6,5},{7,6},{9,8},{10,9},{11,10},{12... | collective-permute-start | bytes 79880 | tf_op jit(solution)/shard_map/ppermute | solution.py:53
  352.2 38.7 %collective-permute-start.52 = (f32[1,1,1,52,6,128]{5,4,3,2,1,0:T(8,128)S(1)}, f32[1,1,1,52,6,128]{5,4,3,2,1,0:T(8,128)S(1)}, u32[]{:S(2)}, u32[]{:S(2)}) collective-permute-start(f32[1,1,1,52,6,128]{5,4,3,2,1,0:T(8,128)S(1)} %get-tuple-element.44), channel_id=1, source_target_pairs={{0,1},{1,2},{2,3},{3,4},{4,5},{5,6},{6,7},{8,9},{9,10},{10,11},{11... | collective-permute-start | bytes 479240 | tf_op jit(solution)/shard_map/ppermute | solution.py:52
  357.9 40.6 %collective-permute-start.53 = (f32[1,1,1,52,6,128]{5,4,3,2,1,0:T(8,128)S(1)}, f32[1,1,1,52,6,128]{5,4,3,2,1,0:T(8,128)S(1)}, u32[]{:S(2)}, u32[]{:S(2)}) collective-permute-start(f32[1,1,1,52,6,128]{5,4,3,2,1,0:T(8,128)S(1)} %get-tuple-element.44), channel_id=1, source_target_pairs={{1,0},{2,1},{3,2},{4,3},{5,4},{6,5},{7,6},{9,8},{10,9},{11,10},{12... | collective-permute-start | bytes 479240 | tf_op jit(solution)/shard_map/ppermute | solution.py:53
  386.4 15.9 %collective-permute-start.42 = (f32[1,1,1,52,128]{4,3,2,1,0:T(8,128)S(1)}, f32[1,1,1,52,128]{4,3,2,1,0:T(8,128)S(1)}, u32[]{:S(2)}, u32[]{:S(2)}) collective-permute-start(f32[1,1,1,52,128]{4,3,2,1,0:T(8,128)S(1)} %bitcast.185), channel_id=1, source_target_pairs={{0,32},{32,64},{64,96},{1,33},{33,65},{65,97},{2,34},{34,66},{66,9... | collective-permute-start | bytes 79880 | tf_op jit(solution)/shard_map/ppermute | solution.py:52
  391.0 14.7 %collective-permute-start.43 = (f32[1,1,1,52,128]{4,3,2,1,0:T(8,128)S(1)}, f32[1,1,1,52,128]{4,3,2,1,0:T(8,128)S(1)}, u32[]{:S(2)}, u32[]{:S(2)}) collective-permute-start(f32[1,1,1,52,128]{4,3,2,1,0:T(8,128)S(1)} %bitcast.186), channel_id=1, source_target_pairs={{32,0},{64,32},{96,64},{33,1},{65,33},{97,65},{34,2},{66,34},{98,6... | collective-permute-start | bytes 79880 | tf_op jit(solution)/shard_map/ppermute | solution.py:53
  392.3 13.4 %collective-permute-start.44 = (f32[1,1,1,52,128]{4,3,2,1,0:T(8,128)S(1)}, f32[1,1,1,52,128]{4,3,2,1,0:T(8,128)S(1)}, u32[]{:S(2)}, u32[]{:S(2)}) collective-permute-start(f32[1,1,1,52,128]{4,3,2,1,0:T(8,128)S(1)} %bitcast.187), channel_id=1, source_target_pairs={{0,8},{8,16},{16,24},{1,9},{9,17},{17,25},{2,10},{10,18},{18,26},{... | collective-permute-start | bytes 79880 | tf_op jit(solution)/shard_map/ppermute | solution.py:52
  397.2 8.4 %collective-permute-start.45 = (f32[1,1,1,52,128]{4,3,2,1,0:T(8,128)S(1)}, f32[1,1,1,52,128]{4,3,2,1,0:T(8,128)S(1)}, u32[]{:S(2)}, u32[]{:S(2)}) collective-permute-start(f32[1,1,1,52,128]{4,3,2,1,0:T(8,128)S(1)} %bitcast.188), channel_id=1, source_target_pairs={{8,0},{16,8},{24,16},{9,1},{17,9},{25,17},{10,2},{18,10},{26,18},{... | collective-permute-start | bytes 79880 | tf_op jit(solution)/shard_map/ppermute | solution.py:53
  398.5 7.1 %collective-permute-start.46 = (f32[1,1,1,52,128]{4,3,2,1,0:T(8,128)S(1)}, f32[1,1,1,52,128]{4,3,2,1,0:T(8,128)S(1)}, u32[]{:S(2)}, u32[]{:S(2)}) collective-permute-start(f32[1,1,1,52,128]{4,3,2,1,0:T(8,128)S(1)} %bitcast.189), channel_id=1, source_target_pairs={{0,1},{1,2},{2,3},{3,4},{4,5},{5,6},{6,7},{8,9},{9,10},{10,11},{11... | collective-permute-start | bytes 79880 | tf_op jit(solution)/shard_map/ppermute | solution.py:52
  402.2 4.9 collective-permute-start.47
  (4 other events, 76.1 us)
where the time goes:
time: 528 us; the launch traced here: 519 us
  matrix products  238 us (45%)
  starting transfers between devices  177 us (34%)
  blocking collectives  40.7 us (8%)
  local copies, waits for them, and re-layouts  36.9 us (7%)
  waiting for transfers between devices  13.3 us (3%)
  between operations  8.1 us (2%)
    dot_general x8, matrix products, local(): mixed = jnp.einsum('bkij,bkj->bi', a_blocks, picked, precision=precise_mode)  198 us
    ppermute x30, starting transfers between devices, extended(): lax.ppermute(last, axis, up)  122 us
    psum x4, blocking collectives, by_axis(): array = lax.psum(array, axis)  40.7 us
    dot_general x1, matrix products, local(): jnp.einsum('bksj,bkij->bksi', picked_p0, a_blocks, precision=precise_mode)  40.1 us
    ppermute x30, starting transfers between devices, extended(): lax.ppermute(leading, axis, [(b, a) for a, b in up])  39.1 us
    all_to_all x3, starting transfers between devices, sent_to_all(): return lax.all_to_all(copies, axis, split_axis=0, concat_axis=0, tiled=True)  16.3 us
  transfers between devices with their start and end apart: 63, of which 7 were waited for; matrix products, arithmetic and copies ran while one was open for 25% of the time, Pallas kernels for 0%

commit v1 on v0

v1 whole, which is shorter than its diff:
```python
import functools

import jax
import jax.numpy as jnp
from jax import lax
from jax.experimental import pallas as pl
from jax.experimental.pallas import tpu as pltpu
from jax.sharding import PartitionSpec as P

ITERS = 8
BR = 52
K = 7
NS = 6
B = 128
G = 4
GROUPS = BR // G
PROWS = 8
NX, NY, NZ = 4, 4, 8
AXES = ("gx", "gy", "gz")
MESH = pl.DeviceIdType.MESH
F32 = jnp.float32


def kernel(
    cols, ids, counts, a_hbm, p0, start,
    prod_hbm, pcols, zlast, norms,
    a_v, x0, x1, acc0, acc1, pt, prod, invd, sq, offs, cg, r1, r2, r3,
    a_sem, xs_sem, xr_sem, ps_sem, pr_sem, out_sem,
    c1s, c1r, c2s, c2r, c3s, c3r, n1s, n1r, n2s, n2r, n3s, n3r,
):
    ix, iy, iz = (lax.axis_index(name) for name in AXES)
    me = (ix * NY + iy) * NZ + iz

    def a_copy(g):
        rows = pl.ds(g * G, G)
        return pltpu.make_async_copy(a_hbm.at[rows], a_v.at[rows], a_sem.at[g])

    for g in range(GROUPS):
        a_copy(g).start()

    def peer_z(d):
        return {"gz": lax.rem(iz + d, NZ)}

    def peer_y(d):
        return {"gy": lax.rem(iy + d, NY)}

    def peer_x(d):
        return {"gx": lax.rem(ix + d, NX)}

    lines = ((peer_z, NZ), (peer_y, NY), (peer_x, NX))

    barrier = pltpu.get_barrier_semaphore()
    for peer, size in lines:
        for d in range(1, size):
            pl.semaphore_signal(barrier, inc=1, device_id=peer(d), device_id_type=MESH)

    def fill(r, carry):
        x0[r] = start[pl.ds(r, 1), :]
        pt[r, 0:NS, :] = p0[r]
        pt[r, NS:8, :] = jnp.full((8 - NS, B), ids[r].astype(F32), F32)
        return carry

    lax.fori_loop(0, BR, fill, 0)
    cg[me] = jnp.full((1, B), counts[0].astype(F32), F32)

    pl.semaphore_wait(barrier, NX + NY + NZ - 3)

    exists = (ix > 0, ix < NX - 1, iy > 0, iy < NY - 1, iz > 0, iz < NZ - 1)
    nearby = (
        {"gx": ix - 1}, {"gx": ix + 1}, {"gy": iy - 1}, {"gy": iy + 1}, {"gz": iz - 1}, {"gz": iz + 1},
    )

    def halo_send(table, send, recv, lo, n):
        for d in range(6):
            @pl.when(exists[d])
            def _(d=d):
                far = d ^ 1
                pltpu.make_async_remote_copy(
                    src_ref=table.at[pl.ds(lo, n)],
                    dst_ref=table.at[pl.ds((far + 1) * BR + lo, n)],
                    send_sem=send.at[d],
                    recv_sem=recv.at[far],
                    device_id=nearby[d],
                    device_id_type=MESH,
                ).start()

    def halo_wait(table, send, recv):
        for d in range(6):
            @pl.when(exists[d])
            def _(d=d):
                copy = pltpu.make_async_remote_copy(
                    src_ref=table.at[pl.ds(0, BR)],
                    dst_ref=table.at[pl.ds((d + 1) * BR, BR)],
                    send_sem=send.at[d],
                    recv_sem=recv.at[d],
                    device_id=nearby[d],
                    device_id_type=MESH,
                )
                copy.wait_recv()
                copy.wait_send()

    def line_copies(ref, peer, size, send, recv):
        return [
            pltpu.make_async_remote_copy(
                src_ref=ref, dst_ref=ref, send_sem=send.at[d - 1], recv_sem=recv.at[d - 1],
                device_id=peer(d), device_id_type=MESH,
            )
            for d in range(1, size)
        ]

    def go(copies):
        for copy in copies:
            copy.start()

    def done(copies):
        for copy in copies:
            copy.wait()

    halo_send(x0, xs_sem.at[0], xr_sem.at[0], 0, BR)
    cg1 = line_copies(cg.at[pl.ds(me, 1)], peer_z, NZ, c1s, c1r)
    cg2 = line_copies(cg.at[pl.ds((ix * NY + iy) * NZ, NZ)], peer_y, NY, c2s, c2r)
    cg3 = line_copies(cg.at[pl.ds(ix * NY * NZ, NY * NZ)], peer_x, NX, c3s, c3r)
    go(cg1)
    halo_send(pt, ps_sem, pr_sem, 0, BR)

    sub = lax.broadcasted_iota(jnp.int32, (B, B), 0)
    lane = lax.broadcasted_iota(jnp.int32, (B, B), 1)

    def multiply(cur, g, acc, first):
        if first:
            a_copy(g).wait()
        for j in range(G):
            b = g * G + j
            total = None
            for k in range(K):
                block = a_v[b, k]
                if first and k == 0:
                    diag = jnp.sum(jnp.where(sub == lane, block, 0.0), axis=0, keepdims=True)
                    invd[b] = 1.0 / diag
                term = block * cur[cols[b, k]]
                total = term if total is None else total + term
            acc[j] = total

    def finish(nxt, g, acc, squares):
        for j in range(G):
            b = g * G + j
            y = jnp.sum(acc[j].T, axis=0, keepdims=True) * invd[b]
            nxt[b] = y
            squares = squares + y * y
        return squares

    def iterate(par, first, last):
        cur, nxt = (x0, x1) if par == 0 else (x1, x0)
        halo_wait(cur, xs_sem.at[par], xr_sem.at[par])
        multiply(cur, 0, acc0, first)

        def pair(i, squares):
            multiply(cur, 2 * i + 1, acc1, first)
            squares = finish(nxt, 2 * i, acc0, squares)
            multiply(cur, 2 * i + 2, acc0, first)
            return finish(nxt, 2 * i + 1, acc1, squares)

        send = functools.partial(halo_send, nxt, xs_sem.at[1 - par], xr_sem.at[1 - par])
        squares = jnp.zeros((1, B), F32)
        half = GROUPS // 4
        squares = lax.fori_loop(0, half, pair, squares)
        if not last:
            send(0, 2 * half * G)
        squares = lax.fori_loop(half, 2 * half, pair, squares)
        if not last:
            send(2 * half * G, 2 * half * G)
        squares = finish(nxt, GROUPS - 1, acc0, squares)
        if not last:
            send(4 * half * G, BR - 4 * half * G)
        return squares

    nt = (((1,), (1,)), ((), ()))

    def p_row(b):
        scale = -invd[b]
        for k in range(K):
            p = pt[cols[b, k]]
            p_hi = p.astype(jnp.bfloat16)
            p_lo = (p - p_hi.astype(F32)).astype(jnp.bfloat16)
            lhs = jnp.concatenate([p_hi, p_lo], axis=0)
            a = a_v[b, k]
            a_hi = a.astype(jnp.bfloat16)
            a_lo = (a - a_hi.astype(F32)).astype(jnp.bfloat16)
            by_hi = lax.dot_general(lhs, a_hi, nt, preferred_element_type=F32)
            by_lo = lax.dot_general(lhs, a_lo, nt, preferred_element_type=F32)
            value = by_hi[0:8] + ((by_hi[8:16] + by_lo[0:8]) + by_lo[8:16])
            prod[b, k] = (value * scale)[0:NS]

    def p_rows(turn):
        first_row = jnp.minimum(PROWS * turn, BR - PROWS)

        def one(r, carry):
            p_row(first_row + r)
            return carry

        lax.fori_loop(0, PROWS, one, 0)

    iterate(0, True, False)
    done(cg1)
    go(cg2)
    halo_wait(pt, ps_sem, pr_sem)

    def two(i, carry):
        p_rows(2 * i)
        iterate(1, False, False)
        p_rows(2 * i + 1)
        sq[...] = iterate(0, False, False)

        @pl.when(i == 0)
        def _():
            done(cg2)
            go(cg3)

        return carry

    lax.fori_loop(0, (ITERS - 2) // 2, two, 0)
    done(cg3)
    p_rows(ITERS - 2)
    out = pltpu.make_async_copy(prod, prod_hbm, out_sem)
    out.start()
    squares = iterate(1, False, True)

    row = lax.broadcasted_iota(jnp.int32, (8, B), 0)
    r1[iz] = jnp.where(row == 0, sq[...], squares)
    red1 = line_copies(r1.at[iz], peer_z, NZ, n1s, n1r)
    go(red1)

    strides = (0, -NY * NZ, NY * NZ, -NZ, NZ, -1, 1)
    table = cg[:, 0, :]
    device = lax.broadcasted_iota(jnp.int32, (NX * NY * NZ, B), 0)
    for f in range(7):
        below = jnp.where(device < me + strides[f], table, 0.0)
        offs[f] = jnp.sum(below, axis=0, keepdims=True)

    def col_row(b):
        spot = lax.broadcasted_iota(jnp.int32, (1, B), 1)
        total = jnp.zeros((1, B), F32)
        for k in range(K):
            c = cols[b, k]
            face = lax.shift_right_logical(c * 1261, 16)
            value = pt[c, NS:NS + 1, :] + offs[face]
            total = jnp.where(spot == k, value, total)
        pcols[b] = (6.0 * total).astype(jnp.int32)

    def col_rows(r, carry):
        for j in range(2):
            col_row(2 * r + j)
        return carry

    lax.fori_loop(0, BR // 2, col_rows, 0)

    def copy_out(r, carry):
        zlast[r] = x0[r]
        return carry

    lax.fori_loop(0, BR, copy_out, 0)

    done(red1)
    r2[iy] = jnp.sum(r1[...], axis=0)
    red2 = line_copies(r2.at[iy], peer_y, NY, n2s, n2r)
    go(red2)
    done(red2)
    r3[ix] = jnp.sum(r2[...], axis=0)
    red3 = line_copies(r3.at[ix], peer_x, NX, n3s, n3r)
    go(red3)
    done(red3)
    total = jnp.sum(r3[...], axis=0)
    norms[...] = jnp.broadcast_to(jnp.sum(total, axis=1, keepdims=True), (8, B))
    out.wait()


def local(a_blocks, block_cols, agg_ids, agg_counts, p0_blocks, start_vec):
    vmem = pl.BlockSpec(memory_space=pltpu.VMEM)
    smem = pl.BlockSpec(memory_space=pltpu.SMEM)
    hbm = pl.BlockSpec(memory_space=pltpu.HBM)
    dma = pltpu.SemaphoreType.DMA
    prod, pcols, zlast, norms = pl.pallas_call(
        kernel,
        out_shape=(
            jax.ShapeDtypeStruct((BR, K, NS, B), F32),
            jax.ShapeDtypeStruct((BR, 1, B), jnp.int32),
            jax.ShapeDtypeStruct((BR, 1, B), F32),
            jax.ShapeDtypeStruct((8, B), F32),
        ),
        in_specs=[smem, smem, smem, hbm, vmem, vmem],
        out_specs=(hbm, vmem, vmem, vmem),
        scratch_shapes=[
            pltpu.VMEM((BR, K, B, B), F32),
            pltpu.VMEM((7 * BR, 1, B), F32),
            pltpu.VMEM((7 * BR, 1, B), F32),
            pltpu.VMEM((G, B, B), F32),
            pltpu.VMEM((G, B, B), F32),
            pltpu.VMEM((7 * BR, 8, B), F32),
            pltpu.VMEM((BR, K, NS, B), F32),
            pltpu.VMEM((BR, 1, B), F32),
            pltpu.VMEM((1, B), F32),
            pltpu.VMEM((7, 1, B), F32),
            pltpu.VMEM((NX * NY * NZ, 1, B), F32),
            pltpu.VMEM((NZ, 8, B), F32),
            pltpu.VMEM((NY, 8, B), F32),
            pltpu.VMEM((NX, 8, B), F32),
            dma((GROUPS,)),
            dma((2, 6)),
            dma((2, 6)),
            dma((6,)),
            dma((6,)),
            dma(()),
            dma((NZ - 1,)), dma((NZ - 1,)),
            dma((NY - 1,)), dma((NY - 1,)),
            dma((NX - 1,)), dma((NX - 1,)),
            dma((NZ - 1,)), dma((NZ - 1,)),
            dma((NY - 1,)), dma((NY - 1,)),
            dma((NX - 1,)), dma((NX - 1,)),
        ],
        compiler_params=pltpu.CompilerParams(
            collective_id=0, has_side_effects=True, vmem_limit_bytes=56 * 1024 * 1024
        ),
        name="prolongator",
    )(block_cols, agg_ids, agg_counts, a_blocks, p0_blocks, start_vec)
    last_norm = jnp.sqrt(norms[1, 0])
    spectral = last_norm / jnp.sqrt(norms[0, 0])
    entries = NX * NY * NZ * BR * B
    power_vec = zlast.reshape(BR, B) * (jnp.sqrt(F32(entries)) / last_norm)
    damping = 4.0 / (3.0 * spectral)
    own = jnp.pad(p0_blocks[:, None], ((0, 0), (0, K - 1), (0, 0), (0, 0)))
    p_blocks = damping * prod + own
    p_cols = pcols.reshape(BR, B)[:, :K]
    return p_blocks, p_cols, power_vec


def solution(mesh):
    placed = (
        P(AXES, None, None, None),
        P(AXES, None),
        P(AXES),
        P(AXES),
        P(AXES, None, None),
        P(AXES, None),
    )
    return jax.shard_map(
        local,
        mesh=mesh,
        in_specs=placed,
        out_specs=(P(AXES, None, None, None), P(AXES, None), P(AXES, None)),
        check_vma=False,
    )
```

time: 528 us -> 76.8 us (0.15); the launches traced: 519 us -> 76.6 us
  matrix products: 238 us -> 0 us
  starting transfers between devices: 177 us -> 0 us
  Pallas kernels: 0 us -> 65.4 us
  blocking collectives: 40.7 us -> 0 us
  local copies, waits for them, and re-layouts: 36.9 us -> 6.82 us
  waiting for transfers between devices: 13.3 us -> 0 us
  between operations: 8.1 us -> 2.78 us
    dot_general x9 -> x0, matrix products: 238 us -> none  [the longest x8 198 us: local(): mixed = jnp.einsum('bkij,bkj->bi', a_blocks, picked, precision=precise_mode)]
    ppermute x60 -> x0, starting transfers between devices: 161 us -> none  [the longest x30 122 us: extended(): lax.ppermute(last, axis, up)]
    pallas_call x0 -> x1, Pallas kernels: none -> 65.4 us  [local(): pl.pallas_call(kernel, out_shape=(jax.ShapeDtypeStruct((BR, K, NS, B), F3...]
    psum x4 -> x0, blocking collectives: 40.7 us -> none  [by_axis(): array = lax.psum(array, axis)]
    gather x21 -> x0, local copies, waits for them, and re-layouts: 17.1 us -> none  [the longest x16 10.3 us: local(): picked = faces_of(operate_wide)[block_cols]]
    all_to_all x3 -> x0, starting transfers between devices: 16.3 us -> none  [sent_to_all(): return lax.all_to_all(copies, axis, split_axis=0, concat_axis=0, tiled=True)]
    ppermute x60 -> x0, waiting for transfers between devices: 9.42 us -> none  [the longest x30 9.34 us: extended(): lax.ppermute(leading, axis, [(b, a) for a, b in up])]
  transfers between devices with their start and end apart: 63 -> 0, of which waited for: 7 -> 0; matrix products, arithmetic and copies ran while one was open for 25% -> 0% of each run, Pallas kernels for 0% -> 0%
where the time goes in v1:
time: 76.8 us; the launch traced here: 76.6 us
  Pallas kernels  65.4 us (85%)
  local copies, waits for them, and re-layouts  6.82 us (9%)
  between operations  2.78 us (4%)
  other arithmetic  1.51 us (2%)
    pallas_call x1, Pallas kernels, local(): pl.pallas_call(kernel, out_shape=(jax.ShapeDtypeStruct((BR, K, NS, B), F3...  65.4 us
    unnamed x12, local copies, waits for them, and re-layouts  5.55 us

profile of v1, /device:TPU:0, one launch (start us, length us, event | category | flops | bytes accessed | tf_op | source)
XLA Modules:
  0.0 76.6 jit_solution(6686125896628215272)
XLA Ops:
  1.3 1.4 %copy.9.cols = s32[52,7]{1,0:T(8,128)} copy(s32[52,7]{0,1:T(8,128)} %param.7) | data formatting | bytes 2912 | tf_op args[1]
  2.7 1.6 %copy.22.p0 = f32[52,6,128]{2,1,0:T(8,128)} copy(f32[52,6,128]{2,0,1:T(8,128)} %param.10) | data formatting | bytes 319488 | tf_op args[4]
  4.3 0.0 copy-start
  4.3 65.4 %prolongator.1 = (f32[52,7,6,128]{3,2,1,0:T(8,128)}, s32[52,1,128]{2,1,0:T(1,128)}, f32[52,1,128]{2,1,0:T(1,128)}, f32[8,128]{1,0:T(8,128)}) custom-call(s32[52,7]{1,0:T(8,128)} %copy.9.cols, s32[52]{0:T(128)} %ids.1, s32[1]{0:T(128)S(6)} %copy.23.counts, f32[52,7,128,128]{3,2,1,0:T(8,128)} %a_hbm.1, f32[52,6,128]{2,1,0:T(8,128)} %copy.22.p0, f32[52,128]{1,0:T(8,128)} %start.1), custom_call_target="tpu_custom_call" | custom-call | tf_op jit(solution)/shard_map/prolongator/pallas_call | solution.py:282
  69.8 1.3 %fusion.1 = (f32[1,1]{1,0:T(1,128)}, f32[1,1]{1,0:T(1,128)}) fusion(f32[8,128]{1,0:T(8,128)} %get-tuple-element.7), kind=kLoop, calls=%fused_computation.6 | loop fusion | bytes 16 | tf_op jit(solution)/shard_map/slice | solution.py:326
  72.5 0.0 copy-done
  72.5 1.5 %pad_add_fusion = f32[52,7,6,128]{3,2,1,0:T(8,128)S(1)} fusion(f32[52,1,6,128]{3,2,1,0:T(8,128)S(1)} %bitcast.11, f32[52,7,6,128]{3,2,1,0:T(8,128)} %get-tuple-element.8, f32[]{:T(128)} %bitcast), kind=kLoop, calls=%fused_computation | loop fusion | flops 559104 | bytes 2396164 | tf_op jit(solution)/shard_map/add | solution.py:331
  74.0 0.0 copy-start.2
  74.0 0.0 copy-start.1
  74.0 1.2 %copy.12 = f32[52,7,6,128]{3,0,2,1:T(8,128)} copy(f32[52,7,6,128]{3,2,1,0:T(8,128)S(1)} %pad_add_fusion) | data formatting | bytes 2236416
  75.2 0.0 copy-done.2
  75.3 0.6 copy.20
  75.9 0.0 copy-done.1
  75.9 0.7 copy.13
  (2 shorter events, 0.0 us)
Async XLA Ops:
  4.3 68.2 %copy-start = (f32[52,6,128]{2,1,0:T(8,128)S(1)}, f32[52,6,128]{2,1,0:T(8,128)}, u32[]{:S(2)}) copy-start(f32[52,6,128]{2,1,0:T(8,128)} %copy.22.p0) | copy-start | bytes 479236
  74.0 1.2 %copy-start.2 = (f32[52,1,128]{2,1,0:T(1,128)S(1)}, f32[52,1,128]{2,1,0:T(1,128)}, u32[]{:S(2)}) copy-start(f32[52,1,128]{2,1,0:T(1,128)} %get-tuple-element.10) | copy-start | bytes 79876
  74.0 1.9 %copy-start.1 = (s32[52,1,128]{2,1,0:T(1,128)S(1)}, s32[52,1,128]{2,1,0:T(1,128)}, u32[]{:S(2)}) copy-start(s32[52,1,128]{2,1,0:T(1,128)} %get-tuple-element.9) | copy-start | bytes 79876

commit v2 on v1

v2 whole, which is shorter than its diff:
```python
import functools

import jax
import jax.numpy as jnp
from jax import lax
from jax.experimental import pallas as pl
from jax.experimental.pallas import tpu as pltpu
from jax.sharding import PartitionSpec as P

ITERS = 8
BR = 52
K = 7
NS = 6
B = 128
G = 8
HALF = 4
FULL = BR // G
PROWS = 7
NX, NY, NZ = 4, 4, 8
AXES = ("gx", "gy", "gz")
MESH = pl.DeviceIdType.MESH
F32 = jnp.float32


def kernel(
    cols_hbm, ids_hbm, counts, a_hbm, p0_hbm, start_hbm,
    prod_out, pcols_out, z_out, norms_out,
    cols, ids, p0, start, a_v, x0, x1, acc, pt, prod, invd, own, sq, offs, cg, r1, r2, r3,
    coltab, pcols, zlast, norms,
    in_sem, a_sem, xs_sem, xr_sem, ps_sem, pr_sem, out_sem,
    c1s, c1r, c2s, c2r, c3s, c3r, n1s, n1r, n2s, n2r, n3s, n3r,
):
    ix, iy, iz = (lax.axis_index(name) for name in AXES)
    me = (ix * NY + iy) * NZ + iz

    small = [
        pltpu.make_async_copy(far, near, in_sem.at[i])
        for i, (far, near) in enumerate(
            ((start_hbm, start), (ids_hbm, ids), (p0_hbm, p0), (cols_hbm, cols))
        )
    ]
    for copy in small:
        copy.start()

    def a_copy(g):
        rows = pl.ds(g * HALF, HALF)
        return pltpu.make_async_copy(a_hbm.at[rows], a_v.at[rows], a_sem.at[g])

    for g in range(BR // HALF):
        a_copy(g).start()

    def peer_z(d):
        return {"gz": lax.rem(iz + d, NZ)}

    def peer_y(d):
        return {"gy": lax.rem(iy + d, NY)}

    def peer_x(d):
        return {"gx": lax.rem(ix + d, NX)}

    lines = ((peer_z, NZ), (peer_y, NY), (peer_x, NX))

    barrier = pltpu.get_barrier_semaphore()
    for peer, size in lines:
        for d in range(1, size):
            pl.semaphore_signal(barrier, inc=1, device_id=peer(d), device_id_type=MESH)

    small[0].wait()
    for r in range(BR):
        x0[r] = start[r:r + 1, :]
    cg[me] = jnp.full((1, B), counts[0].astype(F32), F32)

    pl.semaphore_wait(barrier, NX + NY + NZ - 3)

    exists = (ix > 0, ix < NX - 1, iy > 0, iy < NY - 1, iz > 0, iz < NZ - 1)
    nearby = (
        {"gx": ix - 1}, {"gx": ix + 1}, {"gy": iy - 1}, {"gy": iy + 1}, {"gz": iz - 1}, {"gz": iz + 1},
    )

    def halo_send(table, send, recv, lo, n):
        for d in range(6):
            @pl.when(exists[d])
            def _(d=d):
                far = d ^ 1
                pltpu.make_async_remote_copy(
                    src_ref=table.at[pl.ds(lo, n)],
                    dst_ref=table.at[pl.ds((far + 1) * BR + lo, n)],
                    send_sem=send.at[d],
                    recv_sem=recv.at[far],
                    device_id=nearby[d],
                    device_id_type=MESH,
                ).start()

    def halo_wait(table, send, recv):
        for d in range(6):
            @pl.when(exists[d])
            def _(d=d):
                copy = pltpu.make_async_remote_copy(
                    src_ref=table.at[pl.ds(0, BR)],
                    dst_ref=table.at[pl.ds((d + 1) * BR, BR)],
                    send_sem=send.at[d],
                    recv_sem=recv.at[d],
                    device_id=nearby[d],
                    device_id_type=MESH,
                )
                copy.wait_recv()
                copy.wait_send()

    def line_copies(ref, peer, size, send, recv):
        return [
            pltpu.make_async_remote_copy(
                src_ref=ref, dst_ref=ref, send_sem=send.at[d - 1], recv_sem=recv.at[d - 1],
                device_id=peer(d), device_id_type=MESH,
            )
            for d in range(1, size)
        ]

    def go(copies):
        for copy in copies:
            copy.start()

    def done(copies):
        for copy in copies:
            copy.wait()

    halo_send(x0, xs_sem.at[0], xr_sem.at[0], 0, BR)
    cg1 = line_copies(cg.at[pl.ds(me, 1)], peer_z, NZ, c1s, c1r)
    cg2 = line_copies(cg.at[pl.ds((ix * NY + iy) * NZ, NZ)], peer_y, NY, c2s, c2r)
    cg3 = line_copies(cg.at[pl.ds(ix * NY * NZ, NY * NZ)], peer_x, NX, c3s, c3r)
    go(cg1)

    small[1].wait()
    small[2].wait()

    def fill(r, carry):
        for s in range(NS):
            pt[r, s:s + 1, :] = p0[s, pl.ds(r, 1), :]
        pt[r, NS:8, :] = jnp.full((8 - NS, B), ids[r].astype(F32), F32)
        return carry

    lax.fori_loop(0, BR, fill, 0)
    halo_send(pt, ps_sem, pr_sem, 0, BR)
    small[3].wait()

    sub = lax.broadcasted_iota(jnp.int32, (B, B), 0)
    lane = lax.broadcasted_iota(jnp.int32, (B, B), 1)

    def lane_sums(block):
        return jnp.sum(block.T, axis=0, keepdims=True)

    def multiply(cur, b, first):
        total = None
        for k in range(0 if first else 1, K):
            block = a_v[b, k]
            if first and k == 0:
                diag = jnp.sum(jnp.where(sub == lane, block, 0.0), axis=0, keepdims=True)
                invd[b] = 1.0 / diag
            term = block * cur[cols[k, b]]
            total = term if total is None else total + term
        return total

    def finish(nxt, b, j, first, squares):
        y = lane_sums(acc[j])
        if not first:
            y = y + own[b]
        y = y * invd[b]
        nxt[b] = y
        return squares + y * y

    def iterate(par, first, last):
        cur, nxt = (x0, x1) if par == 0 else (x1, x0)
        halo_wait(cur, xs_sem.at[par], xr_sem.at[par])
        if first:
            a_copy(0).wait()
            a_copy(1).wait()
        for j in range(G):
            acc[j] = multiply(cur, j, first)

        def stage(g, squares):
            if first:
                a_copy(2 * g).wait()
                a_copy(2 * g + 1).wait()
            for j in range(G):
                squares = finish(nxt, (g - 1) * G + j, j, first, squares)
                acc[j] = multiply(cur, g * G + j, first)
            return squares

        send = functools.partial(halo_send, nxt, xs_sem.at[1 - par], xr_sem.at[1 - par])
        squares = jnp.zeros((1, B), F32)
        squares = lax.fori_loop(1, 4, stage, squares)
        if not last:
            send(0, 3 * G)
        squares = lax.fori_loop(4, FULL, stage, squares)
        if first:
            a_copy(2 * FULL).wait()
        for j in range(G):
            squares = finish(nxt, (FULL - 1) * G + j, j, first, squares)
            if j < BR - FULL * G:
                acc[j] = multiply(cur, FULL * G + j, first)
        if not last:
            send(3 * G, 3 * G)
        for j in range(BR - FULL * G):
            squares = finish(nxt, FULL * G + j, j, first, squares)
        if not last:
            send(FULL * G, BR - FULL * G)
        return squares

    nt = (((1,), (1,)), ((), ()))

    def halves(value):
        high = value.astype(jnp.bfloat16)
        return high, (value - high.astype(F32)).astype(jnp.bfloat16)

    def p_row(b):
        scale = -invd[b]
        for k in range(K):
            p_hi, p_lo = halves(pt[cols[k, b]])
            p_all = jnp.concatenate([p_hi, p_lo], axis=0)
            a_all = jnp.concatenate(halves(a_v[b, k]), axis=1)
            value = lax.dot_general(
                jnp.concatenate([p_all, p_all], axis=1), a_all, nt, preferred_element_type=F32
            )
            value = (value[0:8] + value[8:16]) * scale
            for s in range(NS):
                prod[k, s, pl.ds(b, 1), :] = value[s:s + 1]

    def between(cur, turn):
        def one(r, carry):
            p_row(turn * PROWS + r)
            lo = jnp.minimum(r * G, BR - G)
            for j in range(G):
                own[lo + j] = lane_sums(a_v[lo + j, 0] * cur[lo + j])
            return carry

        lax.fori_loop(0, PROWS, one, 0)

    iterate(0, True, False)
    done(cg1)
    go(cg2)
    halo_wait(pt, ps_sem, pr_sem)

    def two(i, carry):
        between(x1, 2 * i)
        iterate(1, False, False)
        between(x0, 2 * i + 1)
        sq[...] = iterate(0, False, False)

        @pl.when(i == 0)
        def _():
            done(cg2)
            go(cg3)

        return carry

    lax.fori_loop(0, (ITERS - 2) // 2, two, 0)
    done(cg3)
    between(x1, ITERS - 2)
    squares = iterate(1, False, True)

    row = lax.broadcasted_iota(jnp.int32, (8, B), 0)
    r1[iz] = jnp.where(row == 0, sq[...], squares)
    red1 = line_copies(r1.at[iz], peer_z, NZ, n1s, n1r)
    go(red1)

    for b in range(PROWS * (ITERS - 1), BR):
        p_row(b)
    out = [pltpu.make_async_copy(prod, prod_out, out_sem.at[0])]
    out[0].start()

    done(red1)
    r2[iy] = jnp.sum(r1[...], axis=0)
    red2 = line_copies(r2.at[iy], peer_y, NY, n2s, n2r)
    go(red2)

    strides = (0, -NY * NZ, NY * NZ, -NZ, NZ, -1, 1)
    table = cg[:, 0, :]
    device = lax.broadcasted_iota(jnp.int32, (NX * NY * NZ, B), 0)
    for f in range(7):
        below = jnp.where(device < me + strides[f], table, 0.0)
        offs[f] = jnp.sum(below, axis=0, keepdims=True)

    def col_rows(r, carry):
        spot = lax.broadcasted_iota(jnp.int32, (1, B), 1)
        for j in range(4):
            b = 4 * r + j
            total = jnp.zeros((1, B), F32)
            for k in range(K):
                c = cols[k, b]
                face = lax.shift_right_logical(c * 1261, 16)
                value = pt[c, NS:NS + 1, :] + offs[face]
                total = jnp.where(spot == k, value, total)
            coltab[pl.ds(b, 1), :] = 6.0 * total
            zlast[pl.ds(b, 1), :] = x0[b]
        return carry

    lax.fori_loop(0, BR // 4, col_rows, 0)
    pcols[...] = coltab[...].T[0:K, 0:BR].astype(jnp.int32)
    out.append(pltpu.make_async_copy(pcols, pcols_out, out_sem.at[1]))
    out.append(pltpu.make_async_copy(zlast, z_out, out_sem.at[2]))
    out[1].start()
    out[2].start()

    done(red2)
    r3[ix] = jnp.sum(r2[...], axis=0)
    red3 = line_copies(r3.at[ix], peer_x, NX, n3s, n3r)
    go(red3)
    done(red3)
    total = jnp.sum(r3[...], axis=0)
    norms[...] = jnp.broadcast_to(jnp.sum(total, axis=1, keepdims=True), (8, B))
    out.append(pltpu.make_async_copy(norms, norms_out, out_sem.at[3]))
    out[3].start()
    for copy in out:
        copy.wait()


def scaled(prod, pcols, z, norms, p0, p_blocks, p_cols, power_vec):
    last_norm = jnp.sqrt(norms[1:2, :])
    spectral = last_norm / jnp.sqrt(norms[0:1, :])
    entries = NX * NY * NZ * BR * B
    power_vec[...] = z[...] * (jnp.sqrt(F32(entries)) / last_norm)
    damping = 4.0 / (3.0 * spectral)
    for k in range(K):
        for s in range(NS):
            value = damping * prod[k, s]
            p_blocks[k, s] = value + p0[s] if k == 0 else value
    p_cols[...] = pcols[...]


def local(a_blocks, block_cols, agg_ids, agg_counts, p0_blocks, start_vec):
    vmem = pl.BlockSpec(memory_space=pltpu.VMEM)
    hbm = pl.BlockSpec(memory_space=pltpu.HBM)
    anywhere = pl.BlockSpec(memory_space=pl.ANY)
    dma = pltpu.SemaphoreType.DMA
    p0_turned = jnp.transpose(p0_blocks, (1, 0, 2))
    shapes = (
        jax.ShapeDtypeStruct((K, NS, BR, B), F32),
        jax.ShapeDtypeStruct((K, BR), jnp.int32),
        jax.ShapeDtypeStruct((BR, B), F32),
    )
    prod, pcols, zlast, norms = pl.pallas_call(
        kernel,
        out_shape=(*shapes, jax.ShapeDtypeStruct((8, B), F32)),
        in_specs=[hbm, hbm, pl.BlockSpec(memory_space=pltpu.SMEM), hbm, hbm, hbm],
        out_specs=(anywhere,) * 4,
        scratch_shapes=[
            pltpu.SMEM((K, BR), jnp.int32),
            pltpu.SMEM((BR,), jnp.int32),
            pltpu.VMEM((NS, BR, B), F32),
            pltpu.VMEM((BR, B), F32),
            pltpu.VMEM((BR, K, B, B), F32),
            pltpu.VMEM((7 * BR, 1, B), F32),
            pltpu.VMEM((7 * BR, 1, B), F32),
            pltpu.VMEM((G, B, B), F32),
            pltpu.VMEM((7 * BR, 8, B), F32),
            pltpu.VMEM((K, NS, BR, B), F32),
            pltpu.VMEM((BR, 1, B), F32),
            pltpu.VMEM((BR, 1, B), F32),
            pltpu.VMEM((1, B), F32),
            pltpu.VMEM((7, 1, B), F32),
            pltpu.VMEM((NX * NY * NZ, 1, B), F32),
            pltpu.VMEM((NZ, 8, B), F32),
            pltpu.VMEM((NY, 8, B), F32),
            pltpu.VMEM((NX, 8, B), F32),
            pltpu.VMEM((B, B), F32),
            pltpu.VMEM((K, BR), jnp.int32),
            pltpu.VMEM((BR, B), F32),
            pltpu.VMEM((8, B), F32),
            dma((4,)),
            dma((BR // HALF,)),
            dma((2, 6)),
            dma((2, 6)),
            dma((6,)),
            dma((6,)),
            dma((4,)),
            dma((NZ - 1,)), dma((NZ - 1,)),
            dma((NY - 1,)), dma((NY - 1,)),
            dma((NX - 1,)), dma((NX - 1,)),
            dma((NZ - 1,)), dma((NZ - 1,)),
            dma((NY - 1,)), dma((NY - 1,)),
            dma((NX - 1,)), dma((NX - 1,)),
        ],
        compiler_params=pltpu.CompilerParams(
            collective_id=0, has_side_effects=True, vmem_limit_bytes=67_043_328
        ),
        name="prolongator",
    )(block_cols.T, agg_ids, agg_counts, a_blocks, p0_turned, start_vec)
    p_blocks, p_cols, power_vec = pl.pallas_call(
        scaled,
        out_shape=shapes,
        in_specs=[vmem] * 5,
        out_specs=(vmem,) * 3,
        name="scaled",
    )(prod, pcols, zlast, norms, p0_turned)
    return jnp.transpose(p_blocks, (2, 0, 1, 3)), p_cols.T, power_vec


def solution(mesh):
    placed = (
        P(AXES, None, None, None),
        P(AXES, None),
        P(AXES),
        P(AXES),
        P(AXES, None, None),
        P(AXES, None),
    )
    return jax.shard_map(
        local,
        mesh=mesh,
        in_specs=placed,
        out_specs=(P(AXES, None, None, None), P(AXES, None), P(AXES, None)),
        check_vma=False,
    )
```

time: 76.8 us -> 68 us (0.89)
  local copies, waits for them, and re-layouts: 6.82 us -> 0 us
  other arithmetic: 1.51 us -> 0 us
  between operations: 2.78 us -> 1.29 us
  Pallas kernels: 65.4 us -> 66.6 us
    unnamed x12 -> x0, local copies, waits for them, and re-layouts: 5.55 us -> none
    add x1 -> x0, other arithmetic: 1.49 us -> none  [local(): p_blocks = damping * prod + own]
    slice x1 -> x0, local copies, waits for them, and re-layouts: 1.27 us -> none  [local(): spectral = last_norm / jnp.sqrt(norms[0, 0])]
    pallas_call x1 -> x2, Pallas kernels: 65.4 us -> 66.6 us  [the longest x1 64.1 us: local(): pl.pallas_call(kernel, out_shape=(*shapes, jax.ShapeDtypeStruct((8, B), F...]
where the time goes in v2:
time: 68 us; the launch traced here: 67.9 us
  Pallas kernels  66.6 us (98%)
  between operations  1.29 us (2%)
    pallas_call x1, Pallas kernels, local(): pl.pallas_call(kernel, out_shape=(*shapes, jax.ShapeDtypeStruct((8, B), F...  64.1 us
    pallas_call x1, Pallas kernels, local(): pl.pallas_call(scaled, out_shape=shapes, in_specs=[vmem] * 5, out_specs=(...  2.44 us

profile of v2, /device:TPU:0, one launch (start us, length us, event | category | flops | bytes accessed | tf_op | source)
XLA Modules:
  0.0 67.9 jit_solution(5500227828420107993)
XLA Ops:
  1.3 64.1 %prolongator.1 = (f32[7,6,52,128]{3,2,1,0:T(8,128)}, s32[7,52]{1,0:T(8,128)}, f32[52,128]{1,0:T(8,128)}, f32[8,128]{1,0:T(8,128)}) custom-call(s32[7,52]{1,0:T(8,128)} %bitcast.6, s32[52]{0:T(128)} %ids_hbm.1, s32[1]{0:T(128)S(6)} %copy.9.counts, f32[52,7,128,128]{3,2,1,0:T(8,128)} %a_hbm.1, f32[6,52,128]{2,1,0:T(8,128)} %bitcast.4, f32[52,128]{1,0:T(8,128)} %start_hbm.1), custom_call_target="tpu_custom_call" | custom-call | tf_op jit(solution)/shard_map/prolongator/pallas_call | solution.py:340
  65.4 2.4 %scaled.1 = (f32[7,6,52,128]{3,2,1,0:T(8,128)}, s32[7,52]{1,0:T(8,128)}, f32[52,128]{1,0:T(8,128)}) custom-call(f32[7,6,52,128]{3,2,1,0:T(8,128)} %get-tuple-element.10.prod, s32[7,52]{1,0:T(8,128)} %get-tuple-element.11.pcols, f32[52,128]{1,0:T(8,128)} %get-tuple-element.12.z, f32[8,128]{1,0:T(8,128)} %get-tuple-element.13.norms, f32[6,52,128]{2,1,0:T(8,128)} %bitcast.5), custom_call_target="tpu_custom_call" | custom-call | tf_op jit(solution)/shard_map/scaled/pallas_call | solution.py:387

commit v3 on v2

--- a/solution.py
+++ b/solution.py
@@ -25,10 +25,10 @@
 def kernel(
     cols_hbm, ids_hbm, counts, a_hbm, p0_hbm, start_hbm,
     prod_out, pcols_out, z_out, norms_out,
-    cols, ids, p0, start, a_v, x0, x1, acc, pt, prod, invd, own, sq, offs, cg, r1, r2, r3,
+    cols, ids, p0, start, a_v, x0, x1, acc, pt, prod, invd, own, sq, offs, cg, r1, r2,
     coltab, pcols, zlast, norms,
     in_sem, a_sem, xs_sem, xr_sem, ps_sem, pr_sem, out_sem,
-    c1s, c1r, c2s, c2r, c3s, c3r, n1s, n1r, n2s, n2r, n3s, n3r,
+    c1s, c1r, c2s, c2r, n1s, n1r, n2s, n2r,
 ):
     ix, iy, iz = (lax.axis_index(name) for name in AXES)
     me = (ix * NY + iy) * NZ + iz
@@ -41,36 +41,38 @@
     ]
     for copy in small:
         copy.start()
+    early = 3
 
     def a_copy(g):
         rows = pl.ds(g * HALF, HALF)
         return pltpu.make_async_copy(a_hbm.at[rows], a_v.at[rows], a_sem.at[g])
 
-    for g in range(BR // HALF):
+
+    for g in range(early):
         a_copy(g).start()
 
     def peer_z(d):
         return {"gz": lax.rem(iz + d, NZ)}
 
-    def peer_y(d):
-        return {"gy": lax.rem(iy + d, NY)}
-
-    def peer_x(d):
-        return {"gx": lax.rem(ix + d, NX)}
-
-    lines = ((peer_z, NZ), (peer_y, NY), (peer_x, NX))
+    def peer_xy(d):
+        return {"gx": lax.rem(ix + d // NY, NX), "gy": lax.rem(iy + d, NY)}
+
+    lines = ((peer_z, NZ), (peer_xy, NX * NY))
 
     barrier = pltpu.get_barrier_semaphore()
     for peer, size in lines:
         for d in range(1, size):
             pl.semaphore_signal(barrier, inc=1, device_id=peer(d), device_id_type=MESH)
 
-    small[0].wait()
+    for copy in small:
+        copy.wait()
+    for g in range(early, BR // HALF):
+        a_copy(g).start()
     for r in range(BR):
         x0[r] = start[r:r + 1, :]
     cg[me] = jnp.full((1, B), counts[0].astype(F32), F32)
 
-    pl.semaphore_wait(barrier, NX + NY + NZ - 3)
+    pl.semaphore_wait(barrier, NX * NY + NZ - 2)
 
     exists = (ix > 0, ix < NX - 1, iy > 0, iy < NY - 1, iz > 0, iz < NZ - 1)
     nearby = (
@@ -125,12 +127,9 @@
 
     halo_send(x0, xs_sem.at[0], xr_sem.at[0], 0, BR)
     cg1 = line_copies(cg.at[pl.ds(me, 1)], peer_z, NZ, c1s, c1r)
-    cg2 = line_copies(cg.at[pl.ds((ix * NY + iy) * NZ, NZ)], peer_y, NY, c2s, c2r)
-    cg3 = line_copies(cg.at[pl.ds(ix * NY * NZ, NY * NZ)], peer_x, NX, c3s, c3r)
+    cg2 = line_copies(cg.at[pl.ds((ix * NY + iy) * NZ, NZ)], peer_xy, NX * NY, c2s, c2r)
     go(cg1)
 
-    small[1].wait()
-    small[2].wait()
 
     def fill(r, carry):
         for s in range(NS):
@@ -140,7 +139,6 @@
 
     lax.fori_loop(0, BR, fill, 0)
     halo_send(pt, ps_sem, pr_sem, 0, BR)
-    small[3].wait()
 
     sub = lax.broadcasted_iota(jnp.int32, (B, B), 0)
     lane = lax.broadcasted_iota(jnp.int32, (B, B), 1)
@@ -245,15 +243,10 @@
         between(x0, 2 * i + 1)
         sq[...] = iterate(0, False, False)
 
-        @pl.when(i == 0)
-        def _():
-            done(cg2)
-            go(cg3)
-
         return carry
 
     lax.fori_loop(0, (ITERS - 2) // 2, two, 0)
-    done(cg3)
+    done(cg2)
     between(x1, ITERS - 2)
     squares = iterate(1, False, True)
 
@@ -268,8 +261,8 @@
     out[0].start()
 
     done(red1)
-    r2[iy] = jnp.sum(r1[...], axis=0)
-    red2 = line_copies(r2.at[iy], peer_y, NY, n2s, n2r)
+    r2[ix * NY + iy] = jnp.sum(r1[...], axis=0)
+    red2 = line_copies(r2.at[ix * NY + iy], peer_xy, NX * NY, n2s, n2r)
     go(red2)
 
     strides = (0, -NY * NZ, NY * NZ, -NZ, NZ, -1, 1)
@@ -301,11 +294,7 @@
     out[2].start()
 
     done(red2)
-    r3[ix] = jnp.sum(r2[...], axis=0)
-    red3 = line_copies(r3.at[ix], peer_x, NX, n3s, n3r)
-    go(red3)
-    done(red3)
-    total = jnp.sum(r3[...], axis=0)
+    total = jnp.sum(r2[...], axis=0)
     norms[...] = jnp.broadcast_to(jnp.sum(total, axis=1, keepdims=True), (8, B))
     out.append(pltpu.make_async_copy(norms, norms_out, out_sem.at[3]))
     out[3].start()
@@ -359,8 +348,7 @@
             pltpu.VMEM((7, 1, B), F32),
             pltpu.VMEM((NX * NY * NZ, 1, B), F32),
             pltpu.VMEM((NZ, 8, B), F32),
-            pltpu.VMEM((NY, 8, B), F32),
-            pltpu.VMEM((NX, 8, B), F32),
+            pltpu.VMEM((NX * NY, 8, B), F32),
             pltpu.VMEM((B, B), F32),
             pltpu.VMEM((K, BR), jnp.int32),
             pltpu.VMEM((BR, B), F32),
@@ -373,11 +361,9 @@
             dma((6,)),
             dma((4,)),
             dma((NZ - 1,)), dma((NZ - 1,)),
-            dma((NY - 1,)), dma((NY - 1,)),
-            dma((NX - 1,)), dma((NX - 1,)),
+            dma((NX * NY - 1,)), dma((NX * NY - 1,)),
             dma((NZ - 1,)), dma((NZ - 1,)),
-            dma((NY - 1,)), dma((NY - 1,)),
-            dma((NX - 1,)), dma((NX - 1,)),
+            dma((NX * NY - 1,)), dma((NX * NY - 1,)),
         ],
         compiler_params=pltpu.CompilerParams(
             collective_id=0, has_side_effects=True, vmem_limit_bytes=67_043_328

time: 68 us -> 62.9 us (0.925)
  Pallas kernels: 66.6 us -> 61.4 us
    pallas_call x1, Pallas kernels: 64.1 us -> 59 us  [local(): pl.pallas_call(kernel, out_shape=(*shapes, jax.ShapeDtypeStruct((8, B), F...]
where the time goes in v3:
time: 62.9 us; the launch traced here: 62.7 us
  Pallas kernels  61.4 us (98%)
  between operations  1.29 us (2%)
    pallas_call x1, Pallas kernels, local(): pl.pallas_call(kernel, out_shape=(*shapes, jax.ShapeDtypeStruct((8, B), F...  59 us
    pallas_call x1, Pallas kernels, local(): pl.pallas_call(scaled, out_shape=shapes, in_specs=[vmem] * 5, out_specs=(...  2.44 us

profile of v3, /device:TPU:0, one launch (start us, length us, event | category | flops | bytes accessed | tf_op | source)
XLA Modules:
  0.0 62.7 jit_solution(12390977204613570265)
XLA Ops:
  1.3 59.0 %prolongator.1 = (f32[7,6,52,128]{3,2,1,0:T(8,128)}, s32[7,52]{1,0:T(8,128)}, f32[52,128]{1,0:T(8,128)}, f32[8,128]{1,0:T(8,128)}) custom-call(s32[7,52]{1,0:T(8,128)} %bitcast.6, s32[52]{0:T(128)} %ids_hbm.1, s32[1]{0:T(128)S(6)} %copy.9.counts, f32[52,7,128,128]{3,2,1,0:T(8,128)} %a_hbm.1, f32[6,52,128]{2,1,0:T(8,128)} %bitcast.4, f32[52,128]{1,0:T(8,128)} %start_hbm.1), custom_call_target="tpu_custom_call" | custom-call | tf_op jit(solution)/shard_map/prolongator/pallas_call | solution.py:329
  60.3 2.4 %scaled.1 = (f32[7,6,52,128]{3,2,1,0:T(8,128)}, s32[7,52]{1,0:T(8,128)}, f32[52,128]{1,0:T(8,128)}) custom-call(f32[7,6,52,128]{3,2,1,0:T(8,128)} %get-tuple-element.10.prod, s32[7,52]{1,0:T(8,128)} %get-tuple-element.11.pcols, f32[52,128]{1,0:T(8,128)} %get-tuple-element.12.z, f32[8,128]{1,0:T(8,128)} %get-tuple-element.13.norms, f32[6,52,128]{2,1,0:T(8,128)} %bitcast.5), custom_call_target="tpu_custom_call" | custom-call | tf_op jit(solution)/shard_map/scaled/pallas_call | solution.py:373

commit v4 on v3

--- a/solution.py
+++ b/solution.py
@@ -15,7 +15,8 @@
 G = 8
 HALF = 4
 FULL = BR // G
-PROWS = 7
+PROWS = 10
+OWN = 6
 NX, NY, NZ = 4, 4, 8
 AXES = ("gx", "gy", "gz")
 MESH = pl.DeviceIdType.MESH
@@ -132,13 +133,12 @@
 
 
     def fill(r, carry):
-        for s in range(NS):
-            pt[r, s:s + 1, :] = p0[s, pl.ds(r, 1), :]
-        pt[r, NS:8, :] = jnp.full((8 - NS, B), ids[r].astype(F32), F32)
+        for j in range(4):
+            b = 4 * r + j
+            for s in range(NS):
+                pt[b, s:s + 1, :] = p0[s, pl.ds(b, 1), :]
+            pt[b, NS:8, :] = jnp.full((8 - NS, B), ids[b].astype(F32), F32)
         return carry
-
-    lax.fori_loop(0, BR, fill, 0)
-    halo_send(pt, ps_sem, pr_sem, 0, BR)
 
     sub = lax.broadcasted_iota(jnp.int32, (B, B), 0)
     lane = lax.broadcasted_iota(jnp.int32, (B, B), 1)
@@ -168,6 +168,17 @@
     def iterate(par, first, last):
         cur, nxt = (x0, x1) if par == 0 else (x1, x0)
         halo_wait(cur, xs_sem.at[par], xr_sem.at[par])
+        send = functools.partial(halo_send, nxt, xs_sem.at[1 - par], xr_sem.at[1 - par])
+        if not first:
+            squares = jnp.zeros((1, B), F32)
+            for lo, hi in ((0, 32), (32, BR)):
+                for b in range(lo, hi):
+                    y = (lane_sums(multiply(cur, b, first)) + own[b]) * invd[b]
+                    nxt[b] = y
+                    squares = squares + y * y
+                if not last:
+                    send(lo, hi - lo)
+            return squares
         if first:
             a_copy(0).wait()
             a_copy(1).wait()
@@ -183,7 +194,6 @@
                 acc[j] = multiply(cur, g * G + j, first)
             return squares
 
-        send = functools.partial(halo_send, nxt, xs_sem.at[1 - par], xr_sem.at[1 - par])
         squares = jnp.zeros((1, B), F32)
         squares = lax.fori_loop(1, 4, stage, squares)
         if not last:
@@ -222,12 +232,21 @@
             for s in range(NS):
                 prod[k, s, pl.ds(b, 1), :] = value[s:s + 1]
 
+    def own_rows(cur, lo, n):
+        for j in range(n):
+            own[lo + j] = lane_sums(a_v[lo + j, 0] * cur[lo + j])
+
+    def own_only(cur):
+        def one(r, carry):
+            own_rows(cur, r * 13, 13)
+            return carry
+
+        lax.fori_loop(0, BR // 13, one, 0)
+
     def between(cur, turn):
         def one(r, carry):
             p_row(turn * PROWS + r)
-            lo = jnp.minimum(r * G, BR - G)
-            for j in range(G):
-                own[lo + j] = lane_sums(a_v[lo + j, 0] * cur[lo + j])
+            own_rows(cur, jnp.minimum(r * OWN, BR - OWN), OWN)
             return carry
 
         lax.fori_loop(0, PROWS, one, 0)
@@ -235,27 +254,49 @@
     iterate(0, True, False)
     done(cg1)
     go(cg2)
-    halo_wait(pt, ps_sem, pr_sem)
 
     def two(i, carry):
-        between(x1, 2 * i)
+        @pl.when(i == 0)
+        def _():
+            lax.fori_loop(0, BR // 4, fill, 0)
+            halo_send(pt, ps_sem, pr_sem, 0, BR // 2)
+            own_only(x1)
+
+        @pl.when(i > 0)
+        def _():
+            between(x1, 2 * i - 2)
+
         iterate(1, False, False)
-        between(x0, 2 * i + 1)
-        sq[...] = iterate(0, False, False)
+
+        @pl.when(i == 0)
+        def _():
+            halo_send(pt, ps_sem, pr_sem, BR // 2, BR // 2)
+            own_only(x0)
+
+        @pl.when(i > 0)
+        def _():
+            between(x0, 2 * i - 1)
+
+        sq[0] = iterate(0, False, False)
+
+        @pl.when(i == 0)
+        def _():
+            halo_wait(pt, ps_sem, pr_sem)
 
         return carry
 
     lax.fori_loop(0, (ITERS - 2) // 2, two, 0)
     done(cg2)
-    between(x1, ITERS - 2)
-    squares = iterate(1, False, True)
-
-    row = lax.broadcasted_iota(jnp.int32, (8, B), 0)
-    r1[iz] = jnp.where(row == 0, sq[...], squares)
+    between(x1, ITERS - 4)
+    sq[1] = iterate(1, False, True)
+
+    both = jnp.sum(sq[...], axis=2, keepdims=True)
+    spot = lax.broadcasted_iota(jnp.int32, (1, B), 1)
+    r1[iz] = jnp.where(spot < B // 2, both[0], both[1])
     red1 = line_copies(r1.at[iz], peer_z, NZ, n1s, n1r)
     go(red1)
 
-    for b in range(PROWS * (ITERS - 1), BR):
+    for b in range(PROWS * (ITERS - 3), BR):
         p_row(b)
     out = [pltpu.make_async_copy(prod, prod_out, out_sem.at[0])]
     out[0].start()
@@ -273,7 +314,6 @@
         offs[f] = jnp.sum(below, axis=0, keepdims=True)
 
     def col_rows(r, carry):
-        spot = lax.broadcasted_iota(jnp.int32, (1, B), 1)
         for j in range(4):
             b = 4 * r + j
             total = jnp.zeros((1, B), F32)
@@ -295,7 +335,7 @@
 
     done(red2)
     total = jnp.sum(r2[...], axis=0)
-    norms[...] = jnp.broadcast_to(jnp.sum(total, axis=1, keepdims=True), (8, B))
+    norms[...] = total
     out.append(pltpu.make_async_copy(norms, norms_out, out_sem.at[3]))
     out[3].start()
     for copy in out:
@@ -303,8 +343,8 @@
 
 
 def scaled(prod, pcols, z, norms, p0, p_blocks, p_cols, power_vec):
-    last_norm = jnp.sqrt(norms[1:2, :])
-    spectral = last_norm / jnp.sqrt(norms[0:1, :])
+    last_norm = jnp.sqrt(norms[:, B - 1:B])
+    spectral = last_norm / jnp.sqrt(norms[:, 0:1])
     entries = NX * NY * NZ * BR * B
     power_vec[...] = z[...] * (jnp.sqrt(F32(entries)) / last_norm)
     damping = 4.0 / (3.0 * spectral)
@@ -328,7 +368,7 @@
     )
     prod, pcols, zlast, norms = pl.pallas_call(
         kernel,
-        out_shape=(*shapes, jax.ShapeDtypeStruct((8, B), F32)),
+        out_shape=(*shapes, jax.ShapeDtypeStruct((1, B), F32)),
         in_specs=[hbm, hbm, pl.BlockSpec(memory_space=pltpu.SMEM), hbm, hbm, hbm],
         out_specs=(anywhere,) * 4,
         scratch_shapes=[
@@ -344,15 +384,15 @@
             pltpu.VMEM((K, NS, BR, B), F32),
             pltpu.VMEM((BR, 1, B), F32),
             pltpu.VMEM((BR, 1, B), F32),
-            pltpu.VMEM((1, B), F32),
+            pltpu.VMEM((2, 1, B), F32),
             pltpu.VMEM((7, 1, B), F32),
             pltpu.VMEM((NX * NY * NZ, 1, B), F32),
-            pltpu.VMEM((NZ, 8, B), F32),
-            pltpu.VMEM((NX * NY, 8, B), F32),
+            pltpu.VMEM((NZ, 1, B), F32),
+            pltpu.VMEM((NX * NY, 1, B), F32),
             pltpu.VMEM((B, B), F32),
             pltpu.VMEM((K, BR), jnp.int32),
             pltpu.VMEM((BR, B), F32),
-            pltpu.VMEM((8, B), F32),
+            pltpu.VMEM((1, B), F32),
             dma((4,)),
             dma((BR // HALF,)),
             dma((2, 6)),

time: 62.9 us -> 59.1 us (0.940)
  Pallas kernels: 61.4 us -> 57.7 us
    pallas_call x1, Pallas kernels: 59 us -> 55.1 us  [local(): pl.pallas_call(kernel, out_shape=(*shapes, jax.ShapeDtypeStruct((1, B), F...]
where the time goes in v4:
time: 59.1 us; the launch traced here: 59 us
  Pallas kernels  57.7 us (98%)
  between operations  1.29 us (2%)
    pallas_call x1, Pallas kernels, local(): pl.pallas_call(kernel, out_shape=(*shapes, jax.ShapeDtypeStruct((1, B), F...  55.1 us
    pallas_call x1, Pallas kernels, local(): pl.pallas_call(scaled, out_shape=shapes, in_specs=[vmem] * 5, out_specs=(...  2.57 us

profile of v4, /device:TPU:0, one launch (start us, length us, event | category | flops | bytes accessed | tf_op | source)
XLA Modules:
  0.0 59.0 jit_solution(250177078355828094)
XLA Ops:
  1.3 55.1 %prolongator.1 = (f32[7,6,52,128]{3,2,1,0:T(8,128)}, s32[7,52]{1,0:T(8,128)}, f32[52,128]{1,0:T(8,128)}, f32[1,128]{1,0:T(1,128)}) custom-call(s32[7,52]{1,0:T(8,128)} %bitcast.6, s32[52]{0:T(128)} %ids_hbm.1, s32[1]{0:T(128)S(6)} %copy.9.counts, f32[52,7,128,128]{3,2,1,0:T(8,128)} %a_hbm.1, f32[6,52,128]{2,1,0:T(8,128)} %bitcast.4, f32[52,128]{1,0:T(8,128)} %start_hbm.1), custom_call_target="tpu_custom_call" | custom-call | tf_op jit(solution)/shard_map/prolongator/pallas_call | solution.py:369
  56.4 2.6 %scaled.1 = (f32[7,6,52,128]{3,2,1,0:T(8,128)}, s32[7,52]{1,0:T(8,128)}, f32[52,128]{1,0:T(8,128)}) custom-call(f32[7,6,52,128]{3,2,1,0:T(8,128)} %get-tuple-element.10.prod, s32[7,52]{1,0:T(8,128)} %get-tuple-element.11.pcols, f32[52,128]{1,0:T(8,128)} %get-tuple-element.12.z, f32[1,128]{1,0:T(1,128)} %get-tuple-element.13.norms, f32[6,52,128]{2,1,0:T(8,128)} %bitcast.5), custom_call_target="tpu_custom_call" | custom-call | tf_op jit(solution)/shard_map/scaled/pallas_call | solution.py:413

commit v5 on v4

--- a/solution.py
+++ b/solution.py
@@ -171,7 +171,7 @@
         send = functools.partial(halo_send, nxt, xs_sem.at[1 - par], xr_sem.at[1 - par])
         if not first:
             squares = jnp.zeros((1, B), F32)
-            for lo, hi in ((0, 32), (32, BR)):
+            for lo, hi in ((0, 40), (40, BR)):
                 for b in range(lo, hi):
                     y = (lane_sums(multiply(cur, b, first)) + own[b]) * invd[b]
                     nxt[b] = y
@@ -342,21 +342,50 @@
         copy.wait()
 
 
-def scaled(prod, pcols, z, norms, p0, p_blocks, p_cols, power_vec):
-    last_norm = jnp.sqrt(norms[:, B - 1:B])
-    spectral = last_norm / jnp.sqrt(norms[:, 0:1])
+def scaled(
+    prod, pcols, z, norms, p0, p_blocks, p_cols, power_vec,
+    prod_v, pcols_v, z_v, norms_v, p0_v, in_sem, out_sem,
+):
+    def taken(i, far, near):
+        return pltpu.make_async_copy(far, near, in_sem.at[i])
+
+    def given(i, near, far):
+        return pltpu.make_async_copy(near, far, out_sem.at[i])
+
+    whole = [
+        taken(K + i, far, near)
+        for i, (far, near) in enumerate(((norms, norms_v), (p0, p0_v), (z, z_v), (pcols, pcols_v)))
+    ]
+    parts = [taken(k, prod.at[k], prod_v.at[k]) for k in range(K)]
+    for copy in whole[:2] + parts + whole[2:]:
+        copy.start()
+    whole[0].wait()
+    last_norm = jnp.sqrt(norms_v[:, B - 1:B])
+    spectral = last_norm / jnp.sqrt(norms_v[:, 0:1])
     entries = NX * NY * NZ * BR * B
-    power_vec[...] = z[...] * (jnp.sqrt(F32(entries)) / last_norm)
+    rescale = jnp.sqrt(F32(entries)) / last_norm
     damping = 4.0 / (3.0 * spectral)
+    whole[1].wait()
+    results = []
     for k in range(K):
+        parts[k].wait()
         for s in range(NS):
-            value = damping * prod[k, s]
-            p_blocks[k, s] = value + p0[s] if k == 0 else value
-    p_cols[...] = pcols[...]
+            value = damping * prod_v[k, s]
+            prod_v[k, s] = value + p0_v[s] if k == 0 else value
+        results.append(given(k, prod_v.at[k], p_blocks.at[k]))
+        results[k].start()
+    whole[2].wait()
+    z_v[...] = z_v[...] * rescale
+    results.append(given(K, z_v, power_vec))
+    results[K].start()
+    whole[3].wait()
+    results.append(given(K + 1, pcols_v, p_cols))
+    results[K + 1].start()
+    for copy in results:
+        copy.wait()
 
 
 def local(a_blocks, block_cols, agg_ids, agg_counts, p0_blocks, start_vec):
-    vmem = pl.BlockSpec(memory_space=pltpu.VMEM)
     hbm = pl.BlockSpec(memory_space=pltpu.HBM)
     anywhere = pl.BlockSpec(memory_space=pl.ANY)
     dma = pltpu.SemaphoreType.DMA
@@ -413,8 +442,18 @@
     p_blocks, p_cols, power_vec = pl.pallas_call(
         scaled,
         out_shape=shapes,
-        in_specs=[vmem] * 5,
-        out_specs=(vmem,) * 3,
+        in_specs=[hbm] * 5,
+        out_specs=(hbm,) * 3,
+        scratch_shapes=[
+            pltpu.VMEM((K, NS, BR, B), F32),
+            pltpu.VMEM((K, BR), jnp.int32),
+            pltpu.VMEM((BR, B), F32),
+            pltpu.VMEM((1, B), F32),
+            pltpu.VMEM((NS, BR, B), F32),
+            dma((K + 4,)),
+            dma((K + 2,)),
+        ],
+        compiler_params=pltpu.CompilerParams(vmem_limit_bytes=67_043_328),
         name="scaled",
     )(prod, pcols, zlast, norms, p0_turned)
     return jnp.transpose(p_blocks, (2, 0, 1, 3)), p_cols.T, power_vec

time: 59.1 us -> 58.6 us (level)
  no operation moved by 1% of the time
where the time goes in v5:
time: 58.6 us; the launch traced here: 58.5 us
  Pallas kernels  57.2 us (98%)
  between operations  1.29 us (2%)
    pallas_call x1, Pallas kernels, local(): pl.pallas_call(kernel, out_shape=(*shapes, jax.ShapeDtypeStruct((1, B), F...  54.9 us
    pallas_call x1, Pallas kernels, local(): pl.pallas_call(scaled, out_shape=shapes, in_specs=[hbm] * 5, out_specs=(h...  2.25 us

profile of v5, /device:TPU:0, one launch (start us, length us, event | category | flops | bytes accessed | tf_op | source)
XLA Modules:
  0.0 58.5 jit_solution(5421131095540265914)
XLA Ops:
  1.3 54.9 %prolongator.1 = (f32[7,6,52,128]{3,2,1,0:T(8,128)}, s32[7,52]{1,0:T(8,128)}, f32[52,128]{1,0:T(8,128)}, f32[1,128]{1,0:T(1,128)}) custom-call(s32[7,52]{1,0:T(8,128)} %bitcast.6, s32[52]{0:T(128)} %ids_hbm.1, s32[1]{0:T(128)S(6)} %copy.9.counts, f32[52,7,128,128]{3,2,1,0:T(8,128)} %a_hbm.1, f32[6,52,128]{2,1,0:T(8,128)} %bitcast.4, f32[52,128]{1,0:T(8,128)} %start_hbm.1), custom_call_target="tpu_custom_call" | custom-call | tf_op jit(solution)/shard_map/prolongator/pallas_call | solution.py:398
  56.2 2.2 %scaled.1 = (f32[7,6,52,128]{3,2,1,0:T(8,128)}, s32[7,52]{1,0:T(8,128)}, f32[52,128]{1,0:T(8,128)}) custom-call(f32[7,6,52,128]{3,2,1,0:T(8,128)} %get-tuple-element.10.prod, s32[7,52]{1,0:T(8,128)} %get-tuple-element.11.pcols, f32[52,128]{1,0:T(8,128)} %get-tuple-element.12.z, f32[1,128]{1,0:T(1,128)} %get-tuple-element.13.norms, f32[6,52,128]{2,1,0:T(8,128)} %bitcast.5), custom_call_target="tpu_custom_call" | custom-call | tf_op jit(solution)/shard_map/scaled/pallas_call | solution.py:442

commit v6 on v5

--- a/solution.py
+++ b/solution.py
@@ -171,7 +171,7 @@
         send = functools.partial(halo_send, nxt, xs_sem.at[1 - par], xr_sem.at[1 - par])
         if not first:
             squares = jnp.zeros((1, B), F32)
-            for lo, hi in ((0, 40), (40, BR)):
+            for lo, hi in ((0, 44), (44, BR)):
                 for b in range(lo, hi):
                     y = (lane_sums(multiply(cur, b, first)) + own[b]) * invd[b]
                     nxt[b] = y

time: 58.6 us -> 58.6 us (level)
  no operation moved by 1% of the time
where the time goes in v6:
time: 58.6 us; the launch traced here: 58.5 us
  Pallas kernels  57.2 us (98%)
  between operations  1.29 us (2%)
    pallas_call x1, Pallas kernels, local(): pl.pallas_call(kernel, out_shape=(*shapes, jax.ShapeDtypeStruct((1, B), F...  55 us
    pallas_call x1, Pallas kernels, local(): pl.pallas_call(scaled, out_shape=shapes, in_specs=[hbm] * 5, out_specs=(h...  2.25 us

profile of v6, /device:TPU:0, one launch (start us, length us, event | category | flops | bytes accessed | tf_op | source)
XLA Modules:
  0.0 58.5 jit_solution(1941687889389474020)
XLA Ops:
  1.3 55.0 %prolongator.1 = (f32[7,6,52,128]{3,2,1,0:T(8,128)}, s32[7,52]{1,0:T(8,128)}, f32[52,128]{1,0:T(8,128)}, f32[1,128]{1,0:T(1,128)}) custom-call(s32[7,52]{1,0:T(8,128)} %bitcast.6, s32[52]{0:T(128)} %ids_hbm.1, s32[1]{0:T(128)S(6)} %copy.9.counts, f32[52,7,128,128]{3,2,1,0:T(8,128)} %a_hbm.1, f32[6,52,128]{2,1,0:T(8,128)} %bitcast.4, f32[52,128]{1,0:T(8,128)} %start_hbm.1), custom_call_target="tpu_custom_call" | custom-call | tf_op jit(solution)/shard_map/prolongator/pallas_call | solution.py:398
  56.3 2.2 %scaled.1 = (f32[7,6,52,128]{3,2,1,0:T(8,128)}, s32[7,52]{1,0:T(8,128)}, f32[52,128]{1,0:T(8,128)}) custom-call(f32[7,6,52,128]{3,2,1,0:T(8,128)} %get-tuple-element.10.prod, s32[7,52]{1,0:T(8,128)} %get-tuple-element.11.pcols, f32[52,128]{1,0:T(8,128)} %get-tuple-element.12.z, f32[1,128]{1,0:T(1,128)} %get-tuple-element.13.norms, f32[6,52,128]{2,1,0:T(8,128)} %bitcast.5), custom_call_target="tpu_custom_call" | custom-call | tf_op jit(solution)/shard_map/scaled/pallas_call | solution.py:442
